TPU v7x, 32 devices: a whole 2x2x4 slice. The times are simulated.
32 devices in a mesh: space: 16 (over z, y, x), rep: 2 (over core).
Axes of the slice: x: 2, y: 2, z: 4, core: 2. Of those that a mesh axis runs over, the one named last changes fastest.
Arguments:
- halo_rows: bfloat16 [4, 2048, 256], P(None, 'space', 'rep'), may hold values from -6 to 6
- unmatched: int32 [4, 2048], P(None, 'space'), may hold values 0 or 1
- owner_id: int32 [4, 2048, 1], P(None, 'space'), may hold values from 0 to 15; in each aligned block of 128 rows (0 to 127, 128 to 255, ..., all dimensions but the last counted through in order) at most 16 rows name the same one
- cand_index: int32 [4, 2048, 16], P(None, 'space'), may hold values from 0 to 511
- lengths: int32 [4, 2048], P(None, 'space'), may hold values from 1 to 16
- choice_index: int32 [4, 2048], P(None, 'space'), may hold values from 0 to 15, as said below
- desc_rows: bfloat16 [4, 8192, 256], P(None, 'space', 'rep'), may hold values from -6 to 6
Outputs:
- phantom: bfloat16 [4, 2048, 256], P(None, 'space', 'rep')
- best_merit: bfloat16 [4, 2048], P(None, 'space')
Inputs may be any that keep to these rules, and one draw needn't show every extreme that they name: `owner_id`: in each aligned block of 128 halos (one region in one snapshot) no owner is named by more than 16 halos, a bound that some block reaches. `choice_index`: less than the halo's length.
All inputs are finite; a program needn't handle non-finite values. No bound on the sum of `unmatched` on one device may be relied on, other than what follows from the above.
Results may differ from a plain program's by a relative error of at most 0.001.
Values may be sent and summed in bfloat16 or wider, within the bound.
No kernel may reach another device: no remote copies, remote signals or barrier semaphores. Data moves between devices by JAX's collectives and lax.ppermute only.
A program may use at most 64 MiB of HBM per device.

v0:
```python
import math

import jax
import jax.numpy as jnp
from jax import lax
from jax.sharding import PartitionSpec as P

WIDTH = 256
K = 16


def route_snapshot(rows_here, live_here, dest_owner, listing, span, picks, peer_count, slot_count):
    slot_total = peer_count * slot_count
    halo_count, half_width = rows_here.shape
    peer_ids = jnp.arange(peer_count, dtype=jnp.int32)
    onehot = (dest_owner[:, None] == peer_ids[None, :]).astype(jnp.bfloat16)
    halo_ids = jnp.arange(halo_count, dtype=jnp.int32)
    lower = (halo_ids[:, None] >= halo_ids[None, :]).astype(jnp.bfloat16)
    prefix = jnp.dot(lower, onehot, preferred_element_type=jnp.float32)
    slot_rank = (jnp.sum(prefix * onehot.astype(jnp.float32), axis=1) - 1.0).astype(jnp.int32)
    target = dest_owner * slot_count + slot_rank
    meta_rows = jnp.concatenate(
        [listing, live_here[:, None], span[:, None], picks[:, None]], axis=1
    )
    send_rows = jnp.zeros((slot_total, half_width), jnp.bfloat16).at[target].set(rows_here)
    send_meta = jnp.zeros((slot_total, K + 3), jnp.int32).at[target].set(meta_rows)
    return (
        send_rows.reshape(peer_count, slot_count, half_width),
        send_meta.reshape(peer_count, slot_count, K + 3),
        target,
    )


def score_requests(got_rows, got_meta, desc_table):
    slot_total, half_width = got_rows.shape
    block_size = min(512, slot_total)
    listed = got_meta[:, :K]

    def score_block(pieces):
        rows_block, index_block = pieces
        tile_scores = jnp.einsum(
            "rw,cw->rc", rows_block, desc_table, preferred_element_type=jnp.float32
        )
        return jnp.take_along_axis(tile_scores, index_block, axis=1)

    partial_merit = lax.map(
        score_block,
        (got_rows.reshape(-1, block_size, half_width), listed.reshape(-1, block_size, K)),
    ).reshape(slot_total, K)
    return partial_merit


def settle_requests(summed, got_rows, got_meta, desc_table, peer_count, slot_count):
    lane_ids = jnp.arange(K, dtype=jnp.int32)
    listed = got_meta[:, :K]
    live_flag = got_meta[:, K]
    length_got = got_meta[:, K + 1]
    pick_pos = got_meta[:, K + 2 : K + 3]
    merit_full = summed / math.sqrt(WIDTH)
    used = lane_ids[None, :] < length_got[:, None]
    live_entry = used & (live_flag[:, None] == 1)
    quality = 1.0 + jax.nn.softplus(merit_full)
    claims = (
        jnp.zeros((desc_table.shape[0],), jnp.float32)
        .at[listed.reshape(-1)]
        .max(jnp.where(live_entry, quality, jnp.zeros_like(quality)).reshape(-1))
    )
    chosen = jnp.take_along_axis(listed, pick_pos, 1)[:, 0]
    chosen_quality = jnp.take_along_axis(quality, pick_pos, 1)[:, 0]
    share_weight = chosen_quality / (chosen_quality + claims[chosen])
    blended = (
        (1.0 - share_weight)[:, None] * got_rows.astype(jnp.float32)
        + share_weight[:, None] * desc_table[chosen].astype(jnp.float32)
    ).astype(jnp.bfloat16)
    top_merit = jnp.max(jnp.where(used, merit_full, jnp.full_like(merit_full, -1e30)), axis=1)
    top_merit = jnp.where(live_flag == 1, top_merit, jnp.zeros_like(top_merit)).astype(jnp.bfloat16)
    return (blended.reshape(peer_count, slot_count, -1), top_merit.reshape(peer_count, slot_count))


def land_replies(back_rows, back_best, target, rows_here, live_here):
    slot_total = back_best.size
    back_rows = back_rows.reshape(slot_total, -1)[target]
    back_best = back_best.reshape(slot_total)[target]
    live_halo = live_here == 1
    return (
        jnp.where(live_halo[:, None], back_rows, rows_here),
        jnp.where(live_halo, back_best, jnp.zeros_like(back_best)),
    )


def body(halo_rows, unmatched, owner_id, cand_index, lengths, choice_index, desc_rows):
    peer_count = lax.axis_size("space")
    snap_count, halo_count, half_width = halo_rows.shape
    slot_count = 2 * halo_count // peer_count
    slot_total = peer_count * slot_count
    phantom_list = []
    best_list = []
    routed = [
        route_snapshot(
            halo_rows[snapshot],
            unmatched[snapshot],
            owner_id[snapshot, :, 0],
            cand_index[snapshot],
            lengths[snapshot],
            choice_index[snapshot],
            peer_count,
            slot_count,
        )
        for snapshot in range(snap_count)
    ]
    all_rows = jnp.stack([item[0] for item in routed])
    all_meta = jnp.stack([item[1] for item in routed])
    got_rows_all, got_meta_all = (
        lax.all_to_all(all_rows, "space", split_axis=1, concat_axis=1, tiled=True),
        lax.all_to_all(all_meta, "space", split_axis=1, concat_axis=1, tiled=True),
    )
    got_rows_all = got_rows_all.reshape(snap_count, slot_total, half_width)
    got_meta_all = got_meta_all.reshape(snap_count, slot_total, K + 3)
    partial_all = jnp.stack(
        [
            score_requests(got_rows_all[snapshot], got_meta_all[snapshot], desc_rows[snapshot])
            for snapshot in range(snap_count)
        ]
    )
    summed_all = lax.psum(partial_all, "rep")
    settled = [
        settle_requests(
            summed_all[snapshot],
            got_rows_all[snapshot],
            got_meta_all[snapshot],
            desc_rows[snapshot],
            peer_count,
            slot_count,
        )
        for snapshot in range(snap_count)
    ]
    blended_all = jnp.stack([item[0] for item in settled])
    top_all = jnp.stack([item[1] for item in settled])
    back_rows_all, back_best_all = (
        lax.all_to_all(blended_all, "space", split_axis=1, concat_axis=1, tiled=True),
        lax.all_to_all(top_all, "space", split_axis=1, concat_axis=1, tiled=True),
    )
    for snapshot in range(snap_count):
        phantom_one, best_one = land_replies(
            back_rows_all[snapshot],
            back_best_all[snapshot],
            routed[snapshot][2],
            halo_rows[snapshot],
            unmatched[snapshot],
        )
        phantom_list.append(phantom_one)
        best_list.append(best_one)
    return (jnp.stack(phantom_list), jnp.stack(best_list))


def solution(mesh):
    in_specs = (
        P(None, "space", "rep"),
        P(None, "space"),
        P(None, "space", None),
        P(None, "space", None),
        P(None, "space"),
        P(None, "space"),
        P(None, "space", "rep"),
    )
    out_specs = (P(None, "space", "rep"), P(None, "space"))
    return jax.shard_map(body, mesh=mesh, in_specs=in_specs, out_specs=out_specs, check_vma=False)
```

profile of v0, /device:TPU:0, one launch (start us, length us, event | category | flops | bytes accessed | tf_op | source)
XLA Modules:
  0.0 399.2 jit_solution(855775819349534204)
XLA Ops:
  10.2 0.9 slice_bitcast_fusion.23
  12.8 0.9 scatter_custom_fusion.4
  13.9 0.9 scatter_custom_fusion.6
  15.1 0.9 scatter_custom_fusion.7
  16.3 0.9 scatter_custom_fusion.5
  18.0 1.1 reshape.1189
  19.1 8.5 %all-to-all-start.1 = ((s32[16,1,1216]{2,1,0:T(1,128)}), s32[16,1,1216]{2,1,0:T(1,128)S(1)}, u32[]{:S(2)}, u32[]{:S(2)}) async-start(s32[16,1,1216]{2,1,0:T(1,128)} %reshape.1189), calls=%async_computation.1 | async-start | bytes 163840 | tf_op jit(solution)/shard_map/all_to_all | solution.py:115
  29.5 0.9 scatter_custom_fusion
  30.4 0.9 scatter_custom_fusion.2
  31.3 0.9 scatter_custom_fusion.3
  32.2 0.9 scatter_custom_fusion.1
  33.9 1.3 all-to-all-done.1
  35.2 5.6 %all-to-all-start = ((bf16[4,16,16,128]{3,2,0,1:T(8,128)(2,1)}), bf16[4,16,16,128]{3,2,0,1:T(8,128)(2,1)S(1)}, u32[]{:S(2)}, u32[]{:S(2)}) async-start(bf16[4,16,16,128]{3,2,0,1:T(8,128)(2,1)} %pad_maximum_fusion), calls=%async_computation | async-start | bytes 524288 | tf_op jit(solution)/shard_map/all_to_all | solution.py:114
  41.5 0.8 reduce.56
  53.5 2.4 gather_fusion.21
  56.0 2.4 gather_fusion.23
  58.4 2.4 gather_fusion.25
  60.8 2.4 gather_fusion.27
  64.8 1.5 gather_fusion.1
  66.3 1.5 gather_fusion.3
  67.8 1.5 gather_fusion.7
  70.6 32.8 %gather_fusion.19 = f32[4096]{0:T(1024)S(1)} fusion(f32[256,512]{1,0:T(8,128)S(1)} %fusion.115, s32[4096]{0:T(1024)S(1)} %reshape.1051), kind=kCustom, calls=%fused_computation.5.clone | custom fusion | bytes 65536 | tf_op jit(solution)/shard_map/while/body/eval_jaxpr/jit(take_along_axis)/gather | solution.py:44
  103.7 32.8 %gather_fusion.16 = f32[4096]{0:T(1024)S(1)} fusion(f32[256,512]{1,0:T(8,128)S(1)} %fusion.112, s32[4096]{0:T(1024)S(1)} %reshape.1036), kind=kCustom, calls=%fused_computation.clone | custom fusion | bytes 65536 | tf_op jit(solution)/shard_map/while/body/eval_jaxpr/jit(take_along_axis)/gather | solution.py:44
  136.9 32.8 %gather_fusion.18 = f32[4096]{0:T(1024)S(1)} fusion(f32[256,512]{1,0:T(8,128)S(1)} %fusion.114, s32[4096]{0:T(1024)S(1)} %reshape.1046), kind=kCustom, calls=%fused_computation.4.clone | custom fusion | bytes 65536 | tf_op jit(solution)/shard_map/while/body/eval_jaxpr/jit(take_along_axis)/gather | solution.py:44
  170.1 32.8 %gather_fusion.17 = f32[4096]{0:T(1024)S(1)} fusion(f32[256,512]{1,0:T(8,128)S(1)} %fusion.113, s32[4096]{0:T(1024)S(1)} %reshape.1041), kind=kCustom, calls=%fused_computation.3.clone | custom fusion | bytes 65536 | tf_op jit(solution)/shard_map/while/body/eval_jaxpr/jit(take_along_axis)/gather | solution.py:44
  203.9 0.9 gather_fusion.5
  204.7 18.3 %all-reduce.2.cloned.1.call-done = f32[4,256,16]{1,2,0:T(8,128)} async-done(((f32[4,256,16]{1,2,0:T(8,128)}), f32[4,256,16]{1,2,0:T(8,128)}) %all-reduce.2.cloned.1.call-update) | async-done | bytes 65552 | tf_op jit(solution)/shard_map/psum | solution.py:125
  223.0 0.8 fusion.63
  223.9 2.4 gather_fusion.20
  226.3 2.4 gather_fusion.22
  228.7 2.4 gather_fusion.26
  231.1 2.4 gather_fusion.24
  234.6 6.8 %all-to-all-start.3 = ((bf16[4,16,16]{2,0,1:T(4,128)(2,1)}), bf16[4,16,16]{2,0,1:T(4,128)(2,1)S(1)}, u32[]{:S(2)}, u32[]{:S(2)}) async-start(bf16[4,16,16]{2,0,1:T(4,128)(2,1)} %pad_maximum_fusion.4), calls=%async_computation.3 | async-start | bytes 32768 | tf_op jit(solution)/shard_map/all_to_all | solution.py:141
  241.8 28.9 %scatter_custom_fusion.8 = f32[512]{0:T(512)S(1)} fusion(s32[4096]{0:T(1024)} %bitcast.383, f32[4096]{0:T(1024)S(1)} %fusion.38, f32[]{:T(128)} %constant.66.clone.1), kind=kCustom, calls=%fused_computation.287 | custom fusion | flops 4096 | bytes 2560 | tf_op jit(solution)/shard_map/scatter-max | solution.py:66
  270.7 2.1 gather_fusion
  274.4 28.9 %scatter_custom_fusion.11 = f32[512]{0:T(512)S(1)} fusion(s32[4096]{0:T(1024)} %bitcast.382, f32[4096]{0:T(1024)S(1)} %fusion.47, f32[]{:T(128)} %constant.66.clone.1), kind=kCustom, calls=%fused_computation.281 | custom fusion | flops 4096 | bytes 2560 | tf_op jit(solution)/shard_map/scatter-max | solution.py:66
  303.3 2.1 gather_fusion.6
  306.5 28.9 %scatter_custom_fusion.10 = f32[512]{0:T(512)S(1)} fusion(s32[4096]{0:T(1024)} %bitcast.381, f32[4096]{0:T(1024)S(1)} %fusion.44, f32[]{:T(128)} %constant.66.clone.1), kind=kCustom, calls=%fused_computation.283 | custom fusion | flops 4096 | bytes 2560 | tf_op jit(solution)/shard_map/scatter-max | solution.py:66
  335.5 1.9 gather_fusion.4
  338.6 28.9 %scatter_custom_fusion.9 = f32[512]{0:T(512)S(1)} fusion(s32[4096]{0:T(1024)} %bitcast.380, f32[4096]{0:T(1024)S(1)} %fusion.41, f32[]{:T(128)} %constant.66.clone.1), kind=kCustom, calls=%fused_computation.285 | custom fusion | flops 4096 | bytes 2560 | tf_op jit(solution)/shard_map/scatter-max | solution.py:66
  367.5 2.1 gather_fusion.2
  371.6 6.9 %all-to-all-start.2 = ((bf16[4,16,16,128]{3,2,0,1:T(8,128)(2,1)}), bf16[4,16,16,128]{3,2,0,1:T(8,128)(2,1)S(1)}, u32[]{:S(2)}, u32[]{:S(2)}) async-start(bf16[4,16,16,128]{3,2,0,1:T(8,128)(2,1)} %pad_maximum_fusion.1), calls=%async_computation.2 | async-start | bytes 524288 | tf_op jit(solution)/shard_map/all_to_all | solution.py:140
  379.0 1.4 gather_fusion.12
  380.3 1.2 gather_fusion.15
  381.6 1.2 gather_fusion.14
  382.8 1.4 gather_fusion.13
  384.8 3.4 all-to-all-done.2
  388.3 1.0 gather_fusion.8
  (295 shorter events, 36.6 us)
Async XLA Ops:
  12.8 17.6 %copy-start.56 = (s32[128]{0:T(128)}, s32[128]{0:T(128)S(1)}, u32[]{:S(2)}) copy-start(s32[128]{0:T(128)S(1)} %get-tuple-element.152) | copy-start | bytes 1540
  12.8 18.5 %copy-start.54 = (s32[128]{0:T(128)}, s32[128]{0:T(128)S(1)}, u32[]{:S(2)}) copy-start(s32[128]{0:T(128)S(1)} %get-tuple-element.151) | copy-start | bytes 1540
  17.9 9.6 %copy-start.24 = (s32[4,128]{1,0:T(4,128)S(1)}, s32[4,128]{1,0:T(4,128)}, u32[]{:S(2)}) copy-start(s32[4,128]{1,0:T(4,128)} %param.14) | copy-start | bytes 6148
  17.9 10.2 %copy-start.13 = (bf16[4,512,128]{2,1,0:T(8,128)(2,1)S(1)}, bf16[4,512,128]{2,1,0:T(8,128)(2,1)}, u32[]{:S(2)}) copy-start(bf16[4,512,128]{2,1,0:T(8,128)(2,1)} %param.19) | copy-start | bytes 1572868
  19.1 10.4 %copy-start.14 = (bf16[4,128,128]{2,1,0:T(8,128)(2,1)S(1)}, bf16[4,128,128]{2,1,0:T(8,128)(2,1)}, u32[]{:S(2)}) copy-start(bf16[4,128,128]{2,1,0:T(8,128)(2,1)} %param.13) | copy-start | bytes 393220
  19.1 16.1 %all-to-all-start.1 = ((s32[16,1,1216]{2,1,0:T(1,128)}), s32[16,1,1216]{2,1,0:T(1,128)S(1)}, u32[]{:S(2)}, u32[]{:S(2)}) async-start(s32[16,1,1216]{2,1,0:T(1,128)} %reshape.1189), calls=%async_computation.1 | async-start | bytes 163840 | tf_op jit(solution)/shard_map/all_to_all | solution.py:115
  35.2 34.7 %all-to-all-start = ((bf16[4,16,16,128]{3,2,0,1:T(8,128)(2,1)}), bf16[4,16,16,128]{3,2,0,1:T(8,128)(2,1)S(1)}, u32[]{:S(2)}, u32[]{:S(2)}) async-start(bf16[4,16,16,128]{3,2,0,1:T(8,128)(2,1)} %pad_maximum_fusion), calls=%async_computation | async-start | bytes 524288 | tf_op jit(solution)/shard_map/all_to_all | solution.py:114
  40.8 182.2 %all-reduce.2.cloned.1.call-start = ((), (), s32[]{:S(2)}) async-start(), calls=%async_computation.4 | async-start | bytes 131072 | tf_op jit(solution)/shard_map/psum | solution.py:125
  43.5 12.4 %copy-start = (s32[256,16]{0,1:T(8,128)}, s32[256,16]{0,1:T(8,128)S(1)}, u32[]{:S(2)}) copy-start(s32[256,16]{0,1:T(8,128)S(1)} %copy.129) | copy-start | bytes 49156
  47.9 19.9 %copy-start.26 = (s32[256,1]{0,1:T(1,128)}, s32[256,1]{0,1:T(1,128)S(1)}, u32[]{:S(2)}) copy-start(s32[256,1]{0,1:T(1,128)S(1)} %copy.140) | copy-start | bytes 3076
  48.0 5.4 %copy-start.38 = (s32[256,1]{0,1:T(1,128)}, s32[256,1]{0,1:T(1,128)S(1)}, u32[]{:S(2)}) copy-start(s32[256,1]{0,1:T(1,128)S(1)} %copy.141) | copy-start | bytes 3076
  49.7 6.2 %copy-start.32 = (s32[256,1]{0,1:T(1,128)}, s32[256,1]{0,1:T(1,128)S(1)}, u32[]{:S(2)}) copy-start(s32[256,1]{0,1:T(1,128)S(1)} %copy.127) | copy-start | bytes 3076
  49.8 6.1 %copy-start.40 = (s32[256,1]{0,1:T(1,128)}, s32[256,1]{0,1:T(1,128)S(1)}, u32[]{:S(2)}) copy-start(s32[256,1]{0,1:T(1,128)S(1)} %copy.132) | copy-start | bytes 3076
  51.5 17.7 %copy-start.30 = (s32[256,1]{0,1:T(1,128)}, s32[256,1]{0,1:T(1,128)S(1)}, u32[]{:S(2)}) copy-start(s32[256,1]{0,1:T(1,128)S(1)} %copy.137) | copy-start | bytes 3076
  51.6 4.3 %copy-start.42 = (s32[256,1]{0,1:T(1,128)}, s32[256,1]{0,1:T(1,128)S(1)}, u32[]{:S(2)}) copy-start(s32[256,1]{0,1:T(1,128)S(1)} %copy.138) | copy-start | bytes 3076
  53.4 5.0 %copy-start.28 = (s32[256,1]{0,1:T(1,128)}, s32[256,1]{0,1:T(1,128)S(1)}, u32[]{:S(2)}) copy-start(s32[256,1]{0,1:T(1,128)S(1)} %copy.134) | copy-start | bytes 3076
  53.5 10.5 %copy-start.44 = (s32[256,1]{0,1:T(1,128)}, s32[256,1]{0,1:T(1,128)S(1)}, u32[]{:S(2)}) copy-start(s32[256,1]{0,1:T(1,128)S(1)} %copy.135) | copy-start | bytes 3076
  53.5 4.8 %copy-start.2 = (s32[256,1]{0,1:T(1,128)}, s32[256,1]{0,1:T(1,128)S(1)}, u32[]{:S(2)}) copy-start(s32[256,1]{0,1:T(1,128)S(1)} %fusion.94) | copy-start | bytes 3076
  56.0 4.8 %copy-start.6 = (s32[256,1]{0,1:T(1,128)}, s32[256,1]{0,1:T(1,128)S(1)}, u32[]{:S(2)}) copy-start(s32[256,1]{0,1:T(1,128)S(1)} %fusion.91) | copy-start | bytes 3076
  58.4 4.8 %copy-start.4 = (s32[256,1]{0,1:T(1,128)}, s32[256,1]{0,1:T(1,128)S(1)}, u32[]{:S(2)}) copy-start(s32[256,1]{0,1:T(1,128)S(1)} %fusion.88) | copy-start | bytes 3076
  60.8 3.3 copy-start.8
  63.2 4.5 %copy-start.46 = (s32[1024]{0:T(1024)}, s32[1024]{0:T(1024)S(1)}, u32[]{:S(2)}) copy-start(s32[1024]{0:T(1024)S(1)} %pad_clamp_fusion.6) | copy-start | bytes 12292
  63.3 4.5 %copy-start.48 = (s32[1024]{0:T(1024)}, s32[1024]{0:T(1024)S(1)}, u32[]{:S(2)}) copy-start(s32[1024]{0:T(1024)S(1)} %pad_clamp_fusion.7) | copy-start | bytes 12292
  170.1 33.0 %copy-start.1 = (s32[256,16]{0,1:T(8,128)S(1)}, s32[256,16]{0,1:T(8,128)}, u32[]{:S(2)}) copy-start(s32[256,16]{0,1:T(8,128)} %copy-done) | copy-start | bytes 49156
  170.1 33.7 %copy-start.49 = (s32[256,1]{0,1:T(1,128)S(1)}, s32[256,1]{0,1:T(1,128)}, u32[]{:S(2)}) copy-start(s32[256,1]{0,1:T(1,128)} %compare_select_fusion.21) | copy-start | bytes 3076
  202.9 20.1 %copy-start.39 = (s32[256,1]{0,1:T(1,128)S(1)}, s32[256,1]{0,1:T(1,128)}, u32[]{:S(2)}) copy-start(s32[256,1]{0,1:T(1,128)} %copy-done.38) | copy-start | bytes 3076
  202.9 20.0 %copy-start.41 = (s32[256,1]{0,1:T(1,128)S(1)}, s32[256,1]{0,1:T(1,128)}, u32[]{:S(2)}) copy-start(s32[256,1]{0,1:T(1,128)} %copy-done.40) | copy-start | bytes 3076
  203.0 20.0 %copy-start.43 = (s32[256,1]{0,1:T(1,128)S(1)}, s32[256,1]{0,1:T(1,128)}, u32[]{:S(2)}) copy-start(s32[256,1]{0,1:T(1,128)} %copy-done.42) | copy-start | bytes 3076
  203.0 20.0 %copy-start.45 = (s32[256,1]{0,1:T(1,128)S(1)}, s32[256,1]{0,1:T(1,128)}, u32[]{:S(2)}) copy-start(s32[256,1]{0,1:T(1,128)} %copy-done.44) | copy-start | bytes 3076
  203.0 20.9 %copy-start.3 = (s32[256,1]{0,1:T(1,128)S(1)}, s32[256,1]{0,1:T(1,128)}, u32[]{:S(2)}) copy-start(s32[256,1]{0,1:T(1,128)} %copy-done.2) | copy-start | bytes 3076
  231.1 10.4 %copy-start.16 = (f32[4,256,16]{1,2,0:T(8,128)S(1)}, f32[4,256,16]{1,2,0:T(8,128)}, u32[]{:S(2)}) copy-start(f32[4,256,16]{1,2,0:T(8,128)} %all-reduce.2.cloned.1.call-done) | copy-start | bytes 196612
  231.1 10.6 %copy-start.37 = (pred[4096]{0:T(1024)(128)(4,1)S(1)}, pred[4096]{0:T(1024)(128)(4,1)}, u32[]{:S(2)}) copy-start(pred[4096]{0:T(1024)(128)(4,1)} %and.77) | copy-start | bytes 12292
  234.6 136.9 %all-to-all-start.3 = ((bf16[4,16,16]{2,0,1:T(4,128)(2,1)}), bf16[4,16,16]{2,0,1:T(4,128)(2,1)S(1)}, u32[]{:S(2)}, u32[]{:S(2)}) async-start(bf16[4,16,16]{2,0,1:T(4,128)(2,1)} %pad_maximum_fusion.4), calls=%async_computation.3 | async-start | bytes 32768 | tf_op jit(solution)/shard_map/all_to_all | solution.py:141
  241.6 31.7 %copy-start.33 = (s32[256,1]{0,1:T(1,128)S(1)}, s32[256,1]{0,1:T(1,128)}, u32[]{:S(2)}) copy-start(s32[256,1]{0,1:T(1,128)} %copy-done.32) | copy-start | bytes 3076
  270.7 3.7 copy-start.34
  274.3 31.2 %copy-start.27 = (s32[256,1]{0,1:T(1,128)S(1)}, s32[256,1]{0,1:T(1,128)}, u32[]{:S(2)}) copy-start(s32[256,1]{0,1:T(1,128)} %copy-done.26) | copy-start | bytes 3076
  306.4 31.1 %copy-start.31 = (s32[256,1]{0,1:T(1,128)S(1)}, s32[256,1]{0,1:T(1,128)}, u32[]{:S(2)}) copy-start(s32[256,1]{0,1:T(1,128)} %copy-done.30) | copy-start | bytes 3076
  338.4 31.2 %copy-start.29 = (s32[256,1]{0,1:T(1,128)S(1)}, s32[256,1]{0,1:T(1,128)}, u32[]{:S(2)}) copy-start(s32[256,1]{0,1:T(1,128)} %copy-done.28) | copy-start | bytes 3076
  338.4 32.0 %copy-start.12 = (bf16[4,16,16,128]{3,2,0,1:T(8,128)(2,1)S(1)}, bf16[4,16,16,128]{3,2,0,1:T(8,128)(2,1)}, u32[]{:S(2)}) copy-start(bf16[4,16,16,128]{3,2,0,1:T(8,128)(2,1)} %copy-done.11) | copy-start | bytes 786436
  338.4 32.0 %copy-start.17 = (bf16[256,128]{1,0:T(8,128)(2,1)S(1)}, bf16[256,128]{1,0:T(8,128)(2,1)}, u32[]{:S(2)}) copy-start(bf16[256,128]{1,0:T(8,128)(2,1)} %gather_fusion.1) | copy-start | bytes 196612
  338.4 32.0 %copy-start.18 = (bf16[256,128]{1,0:T(8,128)(2,1)S(1)}, bf16[256,128]{1,0:T(8,128)(2,1)}, u32[]{:S(2)}) copy-start(bf16[256,128]{1,0:T(8,128)(2,1)} %gather_fusion.3) | copy-start | bytes 196612
  338.4 32.0 %copy-start.19 = (bf16[256,128]{1,0:T(8,128)(2,1)S(1)}, bf16[256,128]{1,0:T(8,128)(2,1)}, u32[]{:S(2)}) copy-start(bf16[256,128]{1,0:T(8,128)(2,1)} %gather_fusion.7) | copy-start | bytes 196612
  370.8 7.7 %copy-start.55 = (s32[128]{0:T(128)S(1)}, s32[128]{0:T(128)}, u32[]{:S(2)}) copy-start(s32[128]{0:T(128)} %copy-done.54) | copy-start | bytes 1540
  370.8 7.7 %copy-start.57 = (s32[128]{0:T(128)S(1)}, s32[128]{0:T(128)}, u32[]{:S(2)}) copy-start(s32[128]{0:T(128)} %copy-done.56) | copy-start | bytes 1540
  371.6 16.6 %all-to-all-start.2 = ((bf16[4,16,16,128]{3,2,0,1:T(8,128)(2,1)}), bf16[4,16,16,128]{3,2,0,1:T(8,128)(2,1)S(1)}, u32[]{:S(2)}, u32[]{:S(2)}) async-start(bf16[4,16,16,128]{3,2,0,1:T(8,128)(2,1)} %pad_maximum_fusion.1), calls=%async_computation.2 | async-start | bytes 524288 | tf_op jit(solution)/shard_map/all_to_all | solution.py:140
  388.2 3.3 copy-start.15
  388.2 3.3 copy-start.50
  388.3 3.3 copy-start.51
  (15 other events, 37.7 us)
Sparse Core Ops, SparseCore 0:
  203.9 18.9 all-reduce.1
where the time goes:
time: 400 us; the launch traced here: 399 us
  local copies, waits for them, and re-layouts  201 us (50%)
  other arithmetic  130 us (32%)
  starting transfers between devices  28 us (7%)
  waiting for transfers between devices  23 us (6%)
  between operations  15.6 us (4%)
    gather x20, local copies, waits for them, and re-layouts, score_block(): return jnp.take_along_axis(tile_scores, index_block, axis=1)  132 us
    another operation x4, other arithmetic, settle_requests(): claims = jnp.zeros((desc_table.shape[0],), jnp.float32).at[listed.reshape...  116 us
    psum x1, waiting for transfers between devices, body(): summed_all = lax.psum(partial_all, 'rep')  18.3 us
    gather x4, local copies, waits for them, and re-layouts, settle_requests(): chosen = jnp.take_along_axis(listed, pick_pos, 1)[:, 0]  9.48 us
    gather x4, local copies, waits for them, and re-layouts, settle_requests(): chosen_quality = jnp.take_along_axis(quality, pick_pos, 1)[:, 0]  9.48 us
    all_to_all x1, starting transfers between devices, body(): lax.all_to_all(all_meta, 'space', split_axis=1, concat_axis=1, tiled=True)  8.47 us
    gather x4, local copies, waits for them, and re-layouts, settle_requests(): share_weight = chosen_quality / (chosen_quality + claims[chosen])  8.19 us
  transfers between devices with their start and end apart: 5, of which 3 were waited for; matrix products, arithmetic and copies ran while one was open for 43% of the time, Pallas kernels for 0%

commit v1 on v0

v1 whole, which is shorter than its diff:
```python
import math

import jax
import jax.numpy as jnp
from jax import lax
from jax.experimental import pallas as pl
from jax.experimental.pallas import tpu as pltpu
from jax.sharding import PartitionSpec as P

LANES = 128
SUB = 8
NEG = -3.0e38


def iota(shape, axis):
    return lax.broadcasted_iota(jnp.int32, shape, axis)


def onehot(mask):
    return jnp.where(mask, 1.0, 0.0).astype(jnp.bfloat16)


def dot(a, b, ca, cb):
    return lax.dot_general(a, b, (((ca,), (cb,)), ((), ())), preferred_element_type=jnp.float32)


class Plan:
    def __init__(self, peers, groups, snaps, halos, width, cands, listed):
        self.peers, self.groups, self.snaps = peers, groups, snaps
        self.halos, self.width, self.cands, self.listed = halos, width, cands, listed
        self.per = snaps // groups
        self.slots = 2 * halos // peers
        self.total = peers * self.slots
        self.data = self.per * self.slots
        self.fit = LANES // listed
        self.send = -(-(self.data + -(-self.data // self.fit)) // SUB) * SUB
        self.back = -(-(self.data + 1) // SUB) * SUB
        self.half = cands // 2
        self.aligned = self.slots % SUB == 0
        assert snaps % groups == 0 and groups == 2
        assert width == LANES and halos <= LANES and cands <= 512
        assert LANES % listed == 0 and self.data <= LANES


def route_kernel(plan, owner_ref, live_ref, cand_ref, span_ref, pick_ref, rows_ref, out_ref, target_ref):
    n, h, k = plan.peers, plan.halos, plan.listed
    rows = n * plan.send
    upper = onehot(iota((h, h), 0) < iota((h, h), 1))
    peer_ids = iota((n, h), 0)
    owners = [owner_ref[s : s + 1, :] for s in range(plan.snaps)]
    marks = jnp.concatenate([onehot(peer_ids == o) for o in owners], axis=0)
    prefix = dot(marks, upper, 1, 0)
    row_ids = iota((rows, h), 0)
    list_ids = iota((k, h), 0)
    for g in range(plan.groups):
        acc = jnp.zeros((rows, plan.width), jnp.float32)
        for q in range(plan.per):
            s = g * plan.per + q
            mine = jnp.where(peer_ids == owners[s], prefix[s * n : (s + 1) * n], 0.0)
            rank = jnp.sum(mine, axis=0, keepdims=True).astype(jnp.int32)
            live = live_ref[s : s + 1, :] == 1
            place = q * plan.slots + rank
            target_ref[s : s + 1, :] = jnp.where(live, owners[s] * LANES + place, -LANES)
            listing = cand_ref[s]
            pick = pick_ref[s : s + 1, :]
            chosen = jnp.sum(jnp.where(list_ids == pick, listing, 0), axis=0, keepdims=True)
            first = listing[0:1, :]
            kept = jnp.where(list_ids < span_ref[s : s + 1, :], listing, chosen)
            kept = jnp.where(list_ids == pick, first, kept)
            kept = jnp.where(list_ids == 0, chosen, kept)
            code = jnp.where(kept < plan.half, kept - plan.half, kept - plan.half + 1)
            code = code.astype(jnp.float32)
            spot = place % plan.fit
            spread = jnp.concatenate(
                [jnp.where(spot == b, code, 0.0) for b in range(plan.fit)], axis=0
            ).astype(jnp.bfloat16)
            data_row = jnp.where(live, owners[s] * plan.send + place, -1)
            meta_row = jnp.where(live, owners[s] * plan.send + plan.data + place // plan.fit, -1)
            acc += dot(onehot(row_ids == data_row), rows_ref[s], 1, 0)
            acc += dot(onehot(row_ids == meta_row), spread, 1, 1)
        out_ref[:, g] = acc.astype(jnp.bfloat16).reshape(n, plan.send, plan.width)


def soft(v):
    return 1.0 + (jnp.maximum(v, 0.0) + jnp.log1p(jnp.exp(-jnp.abs(v))))


def owner_kernel(plan, rep_ref, got_ref, own_ref, other_ref, out_ref):
    n, t, c, k = plan.peers, plan.total, plan.cands, plan.listed
    rep = rep_ref[0]
    scale = 1.0 / math.sqrt(plan.width * plan.groups)
    lane = iota((t, LANES), 1)
    slot_ids = iota((t, 1), 0)
    slot = slot_ids % plan.slots
    source = slot_ids // plan.slots
    col = iota((1, c), 1)
    code = jnp.where(col < plan.half, col - plan.half, col - plan.half + 1).astype(jnp.float32)
    fold = onehot(iota((LANES, k), 0) % k == iota((LANES, k), 1))
    if plan.aligned:
        meta = got_ref[:, 0, plan.data : plan.send, :]
        tall, start = plan.send - plan.data, 0
    else:
        meta = got_ref[:, 0]
        tall, start = plan.send, plan.data
    meta = meta.reshape(n * tall, LANES)
    lanes_of = iota((t, n * tall), 1)
    best_parts = []
    blends = []
    for q in range(plan.per):
        place = q * plan.slots + slot
        pull = onehot(lanes_of == source * tall + start + place // plan.fit)
        wide = dot(pull, meta, 1, 0)
        wide = jnp.where(lane // k == place % plan.fit, wide, 0.0).astype(jnp.bfloat16)
        codes = dot(wide, fold, 1, 0)

        def rows_of(r):
            if plan.aligned:
                piece = got_ref[:, r, q * plan.slots : (q + 1) * plan.slots, :]
                return piece.reshape(t, plan.width)
            whole = got_ref[:, r].reshape(n * plan.send, plan.width)
            take = onehot(iota((t, n * plan.send), 1) == source * plan.send + place)
            return dot(take, whole, 1, 0).astype(jnp.bfloat16)

        rows_own, rows_other = rows_of(rep), rows_of(1 - rep)
        own, other = own_ref[q], other_ref[q]
        merit = (dot(rows_own, own, 1, 1) + dot(rows_other, other, 1, 1)) * scale
        chosen = codes[:, 0:1] == code
        mask = chosen
        for j in range(1, k):
            mask = mask | (codes[:, j : j + 1] == code)
        listed = jnp.where(mask, merit, NEG)
        best = jnp.max(listed, axis=1, keepdims=True)
        top = jnp.max(listed, axis=0, keepdims=True)
        picked = jnp.sum(jnp.where(chosen, merit, 0.0), axis=1, keepdims=True)
        rival = jnp.sum(jnp.where(chosen, top, 0.0), axis=1, keepdims=True)
        mine, claim = soft(picked), soft(rival)
        share = mine / (mine + claim)
        select = onehot(chosen)
        pair = []
        for rows, table in ((rows_own, own), (rows_other, other)):
            desc = dot(select, table, 1, 0)
            pair.append(((1.0 - share) * rows.astype(jnp.float32) + share * desc).astype(jnp.bfloat16))
        blends.append(pair)
        best_parts.append(jnp.where(lane == place, best, 0.0).astype(jnp.bfloat16))
    bests = jnp.concatenate(best_parts, axis=0)
    if plan.aligned:
        tall, start = plan.back - plan.data, 0
    else:
        tall, start = plan.back, plan.data
    where_to = iota((n * tall, plan.per * t), 0)
    source_of = (iota((n * tall, plan.per * t), 1) % t) // plan.slots
    tail = dot(onehot(where_to == source_of * tall + start), bests, 1, 0)
    for i, r in enumerate((rep, 1 - rep)):
        if plan.aligned:
            for q in range(plan.per):
                out_ref[:, r, q * plan.slots : (q + 1) * plan.slots, :] = blends[q][i].reshape(
                    n, plan.slots, plan.width
                )
            out_ref[:, r, plan.data : plan.back, :] = tail.astype(jnp.bfloat16).reshape(n, tall, LANES)
        else:
            both = jnp.concatenate([blends[q][i] for q in range(plan.per)], axis=0)
            item = iota((n * tall, plan.per * t), 1)
            spot = ((item % t) // plan.slots) * tall + (item // t) * plan.slots + item % plan.slots
            full = tail + dot(onehot(where_to == spot), both, 1, 0)
            out_ref[:, r] = full.astype(jnp.bfloat16).reshape(n, tall, LANES)


def land_kernel(plan, back_ref, target_ref, rows_ref, out_ref, best_ref):
    n, h = plan.peers, plan.halos
    tall = n * plan.back
    target = target_ref[...]
    column = jnp.transpose(target)
    if plan.aligned:
        short, start = plan.back - plan.data, 0
    else:
        short, start = plan.back, plan.data
    same = iota((h, h), 0) == iota((h, h), 1)
    for g in range(plan.groups):
        whole = back_ref[:, g].reshape(tall, plan.width)
        if plan.aligned:
            tail = back_ref[:, g, plan.data : plan.back, :].reshape(n * short, LANES)
        else:
            tail = whole
        for q in range(plan.per):
            s = g * plan.per + q
            spot = column[:, s : s + 1]
            owner, place = spot // LANES, spot % LANES
            take = onehot(iota((h, tall), 1) == jnp.where(spot >= 0, owner * plan.back + place, -1))
            keep = onehot(same & (spot < 0))
            out_ref[s] = (dot(take, whole, 1, 0) + dot(keep, rows_ref[s], 1, 0)).astype(jnp.bfloat16)
            spot = target[s : s + 1, :]
            owner, place = spot // LANES, spot % LANES
            pull = onehot(iota((n * short, h), 0) == jnp.where(spot >= 0, owner * short + start, -1))
            grid = dot(tail, pull, 0, 0)
            grid = jnp.where(iota((LANES, h), 0) == place, grid, 0.0)
            best_ref[s : s + 1, :] = jnp.sum(grid, axis=0, keepdims=True).astype(jnp.bfloat16)


def body(halo_rows, unmatched, owner_id, cand_index, lengths, choice_index, desc_rows):
    peers, groups = lax.axis_size("space"), lax.axis_size("rep")
    snaps, halos, width = halo_rows.shape
    cands, listed = desc_rows.shape[1], cand_index.shape[2]
    plan = Plan(peers, groups, snaps, halos, width, cands, listed)
    rep = lax.axis_index("rep").astype(jnp.int32)
    per = plan.per

    other_part = lax.dynamic_slice_in_dim(desc_rows, (1 - rep) * per, per, 0)
    other = lax.ppermute(other_part, "rep", [(0, 1), (1, 0)])
    own = lax.dynamic_slice_in_dim(desc_rows, rep * per, per, 0)

    vmem = pl.BlockSpec(memory_space=pltpu.VMEM)
    smem = pl.BlockSpec(memory_space=pltpu.SMEM)
    sent, target = pl.pallas_call(
        lambda *refs: route_kernel(plan, *refs),
        name="route",
        out_shape=(
            jax.ShapeDtypeStruct((peers, groups, plan.send, width), jnp.bfloat16),
            jax.ShapeDtypeStruct((snaps, halos), jnp.int32),
        ),
        in_specs=[vmem] * 6,
        out_specs=(vmem, vmem),
    )(
        owner_id.reshape(snaps, halos),
        unmatched,
        jnp.swapaxes(cand_index, 1, 2),
        lengths,
        choice_index,
        halo_rows,
    )
    got = lax.all_to_all(
        sent.reshape(peers * groups, plan.send, width), ("space", "rep"), 0, 0, tiled=True
    ).reshape(peers, groups, plan.send, width)
    reply = pl.pallas_call(
        lambda *refs: owner_kernel(plan, *refs),
        name="owner",
        out_shape=jax.ShapeDtypeStruct((peers, groups, plan.back, width), jnp.bfloat16),
        in_specs=[smem, vmem, vmem, vmem],
        out_specs=vmem,
    )(rep.reshape(1), got, own, other)
    back = lax.all_to_all(
        reply.reshape(peers * groups, plan.back, width), ("space", "rep"), 0, 0, tiled=True
    ).reshape(peers, groups, plan.back, width)
    return pl.pallas_call(
        lambda *refs: land_kernel(plan, *refs),
        name="land",
        out_shape=(
            jax.ShapeDtypeStruct((snaps, halos, width), jnp.bfloat16),
            jax.ShapeDtypeStruct((snaps, halos), jnp.bfloat16),
        ),
        in_specs=[vmem] * 3,
        out_specs=(vmem, vmem),
    )(back, target, halo_rows)


def solution(mesh):
    in_specs = (
        P(None, "space", "rep"),
        P(None, "space"),
        P(None, "space", None),
        P(None, "space", None),
        P(None, "space"),
        P(None, "space"),
        P(None, "space", "rep"),
    )
    out_specs = (P(None, "space", "rep"), P(None, "space"))
    return jax.shard_map(body, mesh=mesh, in_specs=in_specs, out_specs=out_specs, check_vma=False)
```

time: 400 us -> 47 us (0.12)
  local copies, waits for them, and re-layouts: 201 us -> 1.48 us
  other arithmetic: 130 us -> 0 us
  starting transfers between devices: 28 us -> 7.58 us
  blocking collectives: 0 us -> 15.3 us
  between operations: 15.6 us -> 0.67 us
  waiting for transfers between devices: 23 us -> 11 us
  Pallas kernels: 0 us -> 10.6 us
    gather x44 -> x0, local copies, waits for them, and re-layouts: 173 us -> none  [the longest x20 132 us: score_block(): return jnp.take_along_axis(tile_scores, index_block, axis=1)]
    another operation x11 -> x0, other arithmetic: 120 us -> none  [the longest x4 116 us: settle_requests(): claims = jnp.zeros((desc_table.shape[0],), jnp.float32).at[listed.reshape...]
    all_to_all x4 -> x1, starting transfers between devices: 27.8 us -> 7.32 us  [body(): lax.all_to_all(sent.reshape(peers * groups, plan.send, width), ('space',...]
    psum x1 -> x0, waiting for transfers between devices: 18.3 us -> none  [body(): summed_all = lax.psum(partial_all, 'rep')]
    all_to_all x0 -> x1, blocking collectives: none -> 15.3 us  [body(): lax.all_to_all(reply.reshape(peers * groups, plan.back, width), ('space',...]
    pallas_call x0 -> x3, Pallas kernels: none -> 10.6 us  [the longest x1 5.98 us: body(): pl.pallas_call(lambda *refs: owner_kernel(plan, *refs), name='owner', out...]
    scatter x8 -> x0, local copies, waits for them, and re-layouts: 7.27 us -> none  [the longest x4 3.65 us: route_snapshot(): jnp.zeros((slot_total, K + 3), jnp.int32).at[target].set(meta_rows)]
    all_to_all x4 -> x1, waiting for transfers between devices: 4.72 us -> 9.74 us  [body(): lax.all_to_all(sent.reshape(peers * groups, plan.send, width), ('space',...]
  transfers between devices with their start and end apart: 5 -> 2, of which waited for: 3 -> 2; matrix products, arithmetic and copies ran while one was open for 43% -> 2% of each run, Pallas kernels for 0% -> 0%
where the time goes in v1:
time: 47 us; the launch traced here: 46.7 us
  blocking collectives  15.3 us (33%)
  waiting for transfers between devices  11 us (23%)
  Pallas kernels  10.6 us (23%)
  starting transfers between devices  7.58 us (16%)
  local copies, waits for them, and re-layouts  1.48 us (3%)
  between operations  0.67 us (1%)
    all_to_all x1, blocking collectives, body(): lax.all_to_all(reply.reshape(peers * groups, plan.back, width), ('space',...  15.3 us
    all_to_all x1, waiting for transfers between devices, body(): lax.all_to_all(sent.reshape(peers * groups, plan.send, width), ('space',...  9.74 us
    all_to_all x1, starting transfers between devices, body(): lax.all_to_all(sent.reshape(peers * groups, plan.send, width), ('space',...  7.32 us
    pallas_call x1, Pallas kernels, body(): pl.pallas_call(lambda *refs: owner_kernel(plan, *refs), name='owner', out...  5.98 us
    pallas_call x1, Pallas kernels, body(): pl.pallas_call(lambda *refs: route_kernel(plan, *refs), name='route', out...  2.44 us
    pallas_call x1, Pallas kernels, body(): pl.pallas_call(lambda *refs: land_kernel(plan, *refs), name='land', out_s...  2.21 us
    ppermute x1, waiting for transfers between devices, body(): other = lax.ppermute(other_part, 'rep', [(0, 1), (1, 0)])  1.28 us
  transfers between devices with their start and end apart: 2, of which 2 were waited for; matrix products, arithmetic and copies ran while one was open for 2% of the time, Pallas kernels for 0%

profile of v1, /device:TPU:0, one launch (start us, length us, event | category | flops | bytes accessed | tf_op | source)
XLA Modules:
  0.0 46.7 jit_solution(1136486905969453234)
XLA Ops:
  0.6 0.0 copy-start.1
  0.6 2.4 %route.1 = (bf16[16,2,40,128]{3,2,1,0:T(8,128)(2,1)}, s32[4,128]{1,0:T(4,128)}) custom-call(s32[4,128]{1,0:T(4,128)} %bitcast.12, s32[4,128]{1,0:T(4,128)} %refs_1_.1, s32[4,16,128]{2,1,0:T(8,128)} %bitcast.11, s32[4,128]{1,0:T(4,128)} %refs_3_.1, s32[4,128]{1,0:T(4,128)} %refs_4_.1, bf16[4,128,128]{2,1,0:T(8,128)(2,1)} %refs_2_.1), custom_call_target="tpu_custom_call" | custom-call | tf_op jit(solution)/shard_map/route/pallas_call | solution.py:213
  3.1 7.3 %all-to-all-start = ((bf16[32,40,128]{2,1,0:T(8,128)(2,1)}), bf16[32,40,128]{2,1,0:T(8,128)(2,1)S(1)}, u32[]{:S(2)}, u32[]{:S(2)}) async-start(bf16[32,40,128]{2,1,0:T(8,128)(2,1)} %bitcast.10), calls=%async_computation | async-start | bytes 655360 | tf_op jit(solution)/shard_map/all_to_all | solution.py:230
  10.4 0.0 copy-done.1
  10.4 0.8 %constant_dynamic-slice_fusion = (bf16[2,512,128]{2,1,0:T(8,128)(2,1)S(1)}, bf16[2,512,128]{2,1,0:T(8,128)(2,1)}) fusion(bf16[4,512,128]{2,1,0:T(8,128)(2,1)S(1)} %copy-done.1, s32[]{:T(128)S(6)} %select_n.7, s32[]{:T(128)S(6)} %select_n.6), kind=kLoop, calls=%fused_computation | loop fusion | bytes 1048584 | tf_op jit(solution)/shard_map/dynamic_slice | solution.py:207
  11.2 0.3 collective-permute-start
  11.4 1.3 %collective-permute-done.refs_3_ = bf16[2,512,128]{2,1,0:T(8,128)(2,1)S(1)} collective-permute-done((bf16[2,512,128]{2,1,0:T(8,128)(2,1)S(1)}, bf16[2,512,128]{2,1,0:T(8,128)(2,1)S(1)}, u32[]{:S(2)}, u32[]{:S(2)}) %collective-permute-start) | collective-permute-done | bytes 262176 | tf_op jit(solution)/shard_map/ppermute | solution.py:208
  12.7 0.0 copy-start.2
  12.7 9.7 %all-to-all-done = bf16[32,40,128]{2,1,0:T(8,128)(2,1)S(1)} async-done(((bf16[32,40,128]{2,1,0:T(8,128)(2,1)}), bf16[32,40,128]{2,1,0:T(8,128)(2,1)S(1)}, u32[]{:S(2)}, u32[]{:S(2)}) %all-to-all-start) | async-done | bytes 327712 | tf_op jit(solution)/shard_map/all_to_all | solution.py:230
  22.5 0.0 copy-start
  22.5 0.0 copy-done.2
  22.5 0.7 %copy-done = bf16[32,40,128]{2,1,0:T(8,128)(2,1)} copy-done((bf16[32,40,128]{2,1,0:T(8,128)(2,1)}, bf16[32,40,128]{2,1,0:T(8,128)(2,1)S(1)}, u32[]{:S(2)}) %copy-start) | copy-done | bytes 327704
  23.2 6.0 %owner.1 = bf16[16,2,40,128]{3,2,1,0:T(8,128)(2,1)} custom-call(s32[1]{0:T(128)} %bitcast.refs_0_, bf16[16,2,40,128]{3,2,1,0:T(8,128)(2,1)} %bitcast.8, bf16[2,512,128]{2,1,0:T(8,128)(2,1)} %get-tuple-element.7.refs_2_, bf16[2,512,128]{2,1,0:T(8,128)(2,1)} %copy-done.2), custom_call_target="tpu_custom_call" | custom-call | tf_op jit(solution)/shard_map/owner/pallas_call | solution.py:233
  29.2 15.3 %all_to_all.10 = bf16[32,40,128]{2,1,0:T(8,128)(2,1)} all-to-all(bf16[32,40,128]{2,1,0:T(8,128)(2,1)} %bitcast.9), channel_id=1, replica_groups=mesh['space'=16,'rep'=2] {'space','rep'}, dimensions={0} | all-to-all | bytes 655360 | tf_op jit(solution)/shard_map/all_to_all | solution.py:240
  44.5 2.2 %land.1 = (bf16[4,128,128]{2,1,0:T(8,128)(2,1)}, bf16[4,128]{1,0:T(4,128)(2,1)}) custom-call(bf16[16,2,40,128]{3,2,1,0:T(8,128)(2,1)} %bitcast.7, s32[4,128]{1,0:T(4,128)} %get-tuple-element.5.refs_1_, bf16[4,128,128]{2,1,0:T(8,128)(2,1)} %refs_2_.1), custom_call_target="tpu_custom_call" | custom-call | tf_op jit(solution)/shard_map/land/pallas_call | solution.py:243
Async XLA Ops:
  0.6 9.8 %copy-start.1 = (bf16[4,512,128]{2,1,0:T(8,128)(2,1)S(1)}, bf16[4,512,128]{2,1,0:T(8,128)(2,1)}, u32[]{:S(2)}) copy-start(bf16[4,512,128]{2,1,0:T(8,128)(2,1)} %param.13) | copy-start | bytes 1572868
  3.1 19.4 %all-to-all-start = ((bf16[32,40,128]{2,1,0:T(8,128)(2,1)}), bf16[32,40,128]{2,1,0:T(8,128)(2,1)S(1)}, u32[]{:S(2)}, u32[]{:S(2)}) async-start(bf16[32,40,128]{2,1,0:T(8,128)(2,1)} %bitcast.10), calls=%async_computation | async-start | bytes 655360 | tf_op jit(solution)/shard_map/all_to_all | solution.py:230
  11.2 1.5 %collective-permute-start = (bf16[2,512,128]{2,1,0:T(8,128)(2,1)S(1)}, bf16[2,512,128]{2,1,0:T(8,128)(2,1)S(1)}, u32[]{:S(2)}, u32[]{:S(2)}) collective-permute-start(bf16[2,512,128]{2,1,0:T(8,128)(2,1)S(1)} %get-tuple-element.6), channel_id=1, source_target_pairs={{0,1},{1,0},{2,3},{3,2},{4,5},{5,4},{6,7},{7,6},{8,9},{9,8},{10,11... | collective-permute-start | bytes 786440 | tf_op jit(solution)/shard_map/ppermute | solution.py:208
  12.7 9.7 %copy-start.2 = (bf16[2,512,128]{2,1,0:T(8,128)(2,1)}, bf16[2,512,128]{2,1,0:T(8,128)(2,1)S(1)}, u32[]{:S(2)}) copy-start(bf16[2,512,128]{2,1,0:T(8,128)(2,1)S(1)} %collective-permute-done.refs_3_) | copy-start | bytes 786436
  22.5 0.7 %copy-start = (bf16[32,40,128]{2,1,0:T(8,128)(2,1)}, bf16[32,40,128]{2,1,0:T(8,128)(2,1)S(1)}, u32[]{:S(2)}) copy-start(bf16[32,40,128]{2,1,0:T(8,128)(2,1)S(1)} %all-to-all-done) | copy-start | bytes 983044

commit v2 on v1

v2 whole, which is shorter than its diff:
```python
import math

import jax
import jax.numpy as jnp
from jax import lax
from jax.experimental import pallas as pl
from jax.experimental.pallas import tpu as pltpu
from jax.sharding import PartitionSpec as P

LANES = 128
SUB = 8
WORD = 32
NEG = -3.0e38


def iota(shape, axis):
    return lax.broadcasted_iota(jnp.int32, shape, axis)


def over(x, m):
    return x >> (m.bit_length() - 1) if m & (m - 1) == 0 else x // m


def left(x, m):
    return x & (m - 1) if m & (m - 1) == 0 else x % m


def onehot(mask):
    return jnp.where(mask, 1.0, 0.0).astype(jnp.bfloat16)


def dot(a, b, ca, cb):
    return lax.dot_general(a, b, (((ca,), (cb,)), ((), ())), preferred_element_type=jnp.float32)


class Plan:
    def __init__(self, peers, groups, snaps, halos, width, cands, listed):
        self.peers, self.groups, self.snaps = peers, groups, snaps
        self.halos, self.width, self.cands, self.listed = halos, width, cands, listed
        self.per = snaps // groups
        self.slots = 2 * halos // peers
        self.total = peers * self.slots
        self.data = self.per * self.slots
        self.fit = LANES // listed
        self.codes = -(-(-(-self.data // self.fit)) // groups)
        self.send = self.data + self.codes + (self.data + self.codes) % 2
        self.back = self.data + 1 + (self.data + 1) % 2
        self.half = cands // 2
        self.aligned = self.slots % SUB == 0
        assert snaps % groups == 0 and groups == 2
        assert width == LANES and halos <= LANES and cands <= 512 and cands % WORD == 0
        assert LANES % listed == 0 and self.data <= LANES
        assert peers * groups * self.send % SUB == 0 and peers * groups * self.back % SUB == 0
        assert not self.aligned or (self.codes <= SUB <= self.data)

    def at(self, peer, group, size):
        return (peer * self.groups + group) * size


def route_kernel(plan, rep_ref, owner_ref, live_ref, cand_ref, span_ref, pick_ref, rows_ref, out_ref, target_ref):
    n, h, k = plan.peers, plan.halos, plan.listed
    rep = rep_ref[0]
    upper = onehot(iota((h, h), 0) < iota((h, h), 1))
    peer_ids = iota((n, h), 0)
    owners = [owner_ref[s : s + 1, :] for s in range(plan.snaps)]
    marks = jnp.concatenate([onehot(peer_ids == o) for o in owners], axis=0)
    prefix = dot(marks, upper, 1, 0)
    list_ids = iota((k, h), 0)
    whole = None
    for g in range(plan.groups):
        rows, tail = None, None
        for q in range(plan.per):
            s = g * plan.per + q
            mine = jnp.where(peer_ids == owners[s], prefix[s * n : (s + 1) * n], 0.0)
            rank = jnp.sum(mine, axis=0, keepdims=True).astype(jnp.int32)
            live = live_ref[s : s + 1, :] == 1
            place = q * plan.slots + rank
            target_ref[s : s + 1, :] = jnp.where(live, owners[s] * LANES + place, -LANES)
            listing = cand_ref[s]
            pick = pick_ref[s : s + 1, :]
            chosen = jnp.sum(jnp.where(list_ids == pick, listing, 0), axis=0, keepdims=True)
            first = listing[0:1, :]
            kept = jnp.where(list_ids < span_ref[s : s + 1, :], listing, chosen)
            kept = jnp.where(list_ids == pick, first, kept)
            kept = jnp.where(list_ids == 0, chosen, kept)
            code = jnp.where(kept < plan.half, kept - plan.half, kept - plan.half + 1)
            code = code.astype(jnp.float32)
            spot, line = left(place, plan.fit), over(place, plan.fit)
            spread = jnp.concatenate(
                [jnp.where(spot == b, code, 0.0) for b in range(plan.fit)], axis=0
            ).astype(jnp.bfloat16)
            tells = live & (over(line, plan.codes) == rep)
            line = left(line, plan.codes)
            if plan.aligned:
                put = iota((n * plan.data, h), 0) == jnp.where(live, owners[s] * plan.data + place, -1)
                say = iota((n * SUB, h), 0) == jnp.where(tells, owners[s] * SUB + line, -1)
            else:
                base = plan.at(owners[s], g, plan.send)
                ids = iota((n * plan.groups * plan.send, h), 0)
                put = ids == jnp.where(live, base + place, -1)
                say = ids == jnp.where(tells, base + plan.data + line, -1)
            part = dot(onehot(put), rows_ref[s], 1, 0)
            note = dot(onehot(say), spread, 1, 1)
            rows = part if rows is None else rows + part
            tail = note if tail is None else tail + note
        if plan.aligned:
            rows, tail = rows.astype(jnp.bfloat16), tail.astype(jnp.bfloat16)
            for p in range(n):
                base = plan.at(p, g, plan.send)
                out_ref[base : base + plan.data, :] = rows[p * plan.data : (p + 1) * plan.data]
                out_ref[base + plan.data : base + plan.send, :] = tail[p * SUB : p * SUB + plan.send - plan.data]
        else:
            both = rows + tail
            whole = both if whole is None else whole + both
    if not plan.aligned:
        out_ref[...] = whole.astype(jnp.bfloat16)


def soft(v):
    return 1.0 + (jnp.maximum(v, 0.0) + jnp.log1p(jnp.exp(-jnp.abs(v))))


def rows_in(plan, ref, group, q, size):
    if plan.aligned:
        starts = [plan.at(p, group, size) + q * plan.slots for p in range(plan.peers)]
        return jnp.concatenate([ref[a : a + plan.slots, :] for a in starts], axis=0)
    shape = (plan.total, plan.peers * plan.groups * size)
    item = iota(shape, 0)
    spot = plan.at(over(item, plan.slots), group, size) + q * plan.slots + left(item, plan.slots)
    return dot(onehot(iota(shape, 1) == spot), ref[...], 1, 0).astype(jnp.bfloat16)


def tail_in(plan, ref, group, size):
    if plan.aligned:
        ends = [plan.at(p, group, size) + size for p in range(plan.peers)]
        value = jnp.concatenate([ref[a - SUB : a, :] for a in ends], axis=0)
        return value, (lambda p: p * SUB + SUB - (size - plan.data))
    return ref[...], (lambda p: plan.at(p, group, size) + plan.data)


def owner_kernel(plan, rep_ref, got_ref, own_ref, other_ref, out_ref):
    n, t, c, k = plan.peers, plan.total, plan.cands, plan.listed
    first = rep_ref[0] == 0
    scale = 1.0 / math.sqrt(plan.width * plan.groups)
    item = iota((1, t), 1)
    source, slot = over(item, plan.slots), left(item, plan.slots)
    snaps, cores = range(plan.per), range(plan.groups)
    ends = [tail_in(plan, got_ref, r, plan.send) for r in cores]

    listing = []
    for q in snaps:
        place = q * plan.slots + slot
        spot, line = left(place, plan.fit), over(place, plan.fit)
        wide = None
        for r in cores:
            value, row = ends[r]
            if (q * plan.slots + plan.slots - 1) // plan.fit // plan.codes < r:
                continue
            if q * plan.slots // plan.fit // plan.codes > r:
                continue
            told = jnp.where(over(line, plan.codes) == r, row(source) + left(line, plan.codes), -1)
            piece = dot(value, onehot(iota((value.shape[0], t), 0) == told), 0, 0)
            wide = piece if wide is None else wide + piece
        codes = None
        for b in range(plan.fit):
            piece = jnp.where(spot == b, wide[b * k : (b + 1) * k], 0.0)
            codes = piece if codes is None else codes + piece
        codes = codes.astype(jnp.int32)
        index = jnp.where(codes < 0, codes + plan.half, codes + plan.half - 1)
        listing.append(jnp.where(codes == 0, -1, index))

    tables = [
        [jnp.where(first, own_ref[q], other_ref[q]), jnp.where(first, other_ref[q], own_ref[q])] for q in snaps
    ]
    rows = [[rows_in(plan, got_ref, r, q, plan.send) for r in cores] for q in snaps]
    merits = [sum(dot(tables[q][r], rows[q][r], 1, 1) for r in cores) for q in snaps]

    words = c // WORD
    word_ids = iota((words, t), 0)
    bits = jnp.left_shift(jnp.int32(1), iota((WORD, t), 0))
    heads = [listing[q][0:1, :].astype(jnp.float32) for q in snaps]
    heads = jnp.transpose(jnp.concatenate(heads + [jnp.zeros((SUB - plan.per, t), jnp.float32)], axis=0))
    heads = heads.astype(jnp.int32)
    bests, shares = [], []
    for q in snaps:
        index = listing[q]
        high, bit = index >> 5, jnp.left_shift(jnp.int32(1), index & (WORD - 1))
        sets = jnp.zeros((words, t), jnp.int32)
        for j in range(k):
            sets = sets | jnp.where(high[j : j + 1, :] == word_ids, bit[j : j + 1, :], 0)
        parts = []
        for w in range(words):
            member = (sets[w : w + 1, :] & bits) != 0
            parts.append(jnp.where(member, merits[q][w * WORD : (w + 1) * WORD], NEG))
        listed = jnp.concatenate(parts, axis=0)
        bests.append(jnp.max(listed, axis=0, keepdims=True) * scale)
        top = jnp.max(listed, axis=1, keepdims=True)
        chosen = iota((c, t), 0) == index[0:1, :]
        picked = jnp.sum(jnp.where(chosen, merits[q], 0.0), axis=0, keepdims=True) * scale
        rival = jnp.sum(jnp.where(chosen, top, 0.0), axis=0, keepdims=True) * scale
        mine, claim = soft(picked), soft(rival)
        shares.append(mine / (mine + claim))
    shares = jnp.transpose(jnp.concatenate(shares + [jnp.zeros((SUB - plan.per, t), jnp.float32)], axis=0))

    blends = []
    for q in snaps:
        select = onehot(iota((t, c), 1) == heads[:, q : q + 1])
        share = shares[:, q : q + 1]
        pair = []
        for r in cores:
            desc = dot(select, tables[q][r], 1, 0)
            pair.append(((1.0 - share) * rows[q][r].astype(jnp.float32) + share * desc).astype(jnp.bfloat16))
        blends.append(pair)

    tail = None
    lane = iota((t, LANES), 1)
    for q in snaps:
        if plan.aligned:
            shape = (n * SUB, t)
            home = source * SUB
        else:
            shape = (n * plan.back, t)
            home = source * plan.back + plan.data
        line = jnp.where(iota(shape, 0) == home, jnp.maximum(bests[q], NEG), 0.0).astype(jnp.bfloat16)
        piece = dot(line, onehot(lane == q * plan.slots + left(iota((t, LANES), 0), plan.slots)), 1, 0)
        tail = piece if tail is None else tail + piece
    if plan.aligned:
        tail = tail.astype(jnp.bfloat16)
        for r in cores:
            for p in range(n):
                base = plan.at(p, r, plan.back)
                for q in snaps:
                    a = base + q * plan.slots
                    out_ref[a : a + plan.slots, :] = blends[q][r][p * plan.slots : (p + 1) * plan.slots]
                out_ref[base + plan.data : base + plan.back, :] = tail[p * SUB : p * SUB + plan.back - plan.data]
        return
    shape = (n * plan.groups * plan.back, t)
    item = iota(shape, 1)
    peer, slot = over(item, plan.slots), left(item, plan.slots)
    shape_tail = (n * plan.groups * plan.back, n * plan.back)
    row, col = iota(shape_tail, 0), iota(shape_tail, 1)
    peer_of, line_of = col // plan.back, col % plan.back
    full = None
    for r in cores:
        copy = onehot(row == plan.at(peer_of, r, plan.back) + line_of)
        piece = dot(copy, tail.astype(jnp.bfloat16), 1, 0)
        for q in snaps:
            put = onehot(iota(shape, 0) == plan.at(peer, r, plan.back) + q * plan.slots + slot)
            piece = piece + dot(put, blends[q][r], 1, 0)
        full = piece if full is None else full + piece
    out_ref[...] = full.astype(jnp.bfloat16)


def land_kernel(plan, back_ref, target_ref, rows_ref, out_ref, best_ref):
    h = plan.halos
    target = target_ref[...]
    column = jnp.transpose(target)
    same = iota((h, h), 0) == iota((h, h), 1)
    for g in range(plan.groups):
        tail, row = tail_in(plan, back_ref, g, plan.back)
        for q in range(plan.per):
            s = g * plan.per + q
            spot = column[:, s : s + 1]
            owner, slot = spot >> 7, (spot & (LANES - 1)) - q * plan.slots
            rows = rows_in(plan, back_ref, g, q, plan.back)
            where_from = jnp.where(spot >= 0, owner * plan.slots + slot, -1)
            take = onehot(iota((h, plan.total), 1) == where_from)
            keep = onehot(same & (spot < 0))
            out_ref[s] = (dot(take, rows, 1, 0) + dot(keep, rows_ref[s], 1, 0)).astype(jnp.bfloat16)
            spot = target[s : s + 1, :]
            owner, place = spot >> 7, spot & (LANES - 1)
            pull = onehot(iota((tail.shape[0], h), 0) == jnp.where(spot >= 0, row(owner), -1))
            grid = dot(tail, pull, 0, 0)
            grid = jnp.where(iota((LANES, h), 0) == place, grid, 0.0)
            best_ref[s : s + 1, :] = jnp.sum(grid, axis=0, keepdims=True).astype(jnp.bfloat16)


def body(halo_rows, unmatched, owner_id, cand_index, lengths, choice_index, desc_rows):
    peers, groups = lax.axis_size("space"), lax.axis_size("rep")
    snaps, halos, width = halo_rows.shape
    cands, listed = desc_rows.shape[1], cand_index.shape[2]
    plan = Plan(peers, groups, snaps, halos, width, cands, listed)
    rep = lax.axis_index("rep").astype(jnp.int32)
    per = plan.per

    def swap(flat, size):
        boxed = flat.reshape(peers * groups, size // 2, 2, width)
        boxed = lax.all_to_all(boxed, ("space", "rep"), 0, 0, tiled=True)
        return boxed.reshape(peers * groups * size, width)

    other_part = lax.dynamic_slice_in_dim(desc_rows, (1 - rep) * per, per, 0)
    other = lax.ppermute(other_part, "rep", [(0, 1), (1, 0)])
    own = lax.dynamic_slice_in_dim(desc_rows, rep * per, per, 0)

    vmem = pl.BlockSpec(memory_space=pltpu.VMEM)
    smem = pl.BlockSpec(memory_space=pltpu.SMEM)
    small = pltpu.CompilerParams(vmem_limit_bytes=20 << 20)
    sent, target = pl.pallas_call(
        lambda *refs: route_kernel(plan, *refs),
        name="route",
        out_shape=(
            jax.ShapeDtypeStruct((peers * groups * plan.send, width), jnp.bfloat16),
            jax.ShapeDtypeStruct((snaps, halos), jnp.int32),
        ),
        in_specs=[smem] + [vmem] * 6,
        out_specs=(vmem, vmem),
    )(
        rep.reshape(1),
        owner_id.reshape(snaps, halos),
        unmatched,
        jnp.swapaxes(cand_index, 1, 2),
        lengths,
        choice_index,
        halo_rows,
    )
    got = swap(sent, plan.send)
    reply = pl.pallas_call(
        lambda *refs: owner_kernel(plan, *refs),
        name="owner",
        compiler_params=small,
        out_shape=jax.ShapeDtypeStruct((peers * groups * plan.back, width), jnp.bfloat16),
        in_specs=[smem, vmem, vmem, vmem],
        out_specs=vmem,
    )(rep.reshape(1), got, own, other)
    back = swap(reply, plan.back)
    return pl.pallas_call(
        lambda *refs: land_kernel(plan, *refs),
        name="land",
        compiler_params=small,
        out_shape=(
            jax.ShapeDtypeStruct((snaps, halos, width), jnp.bfloat16),
            jax.ShapeDtypeStruct((snaps, halos), jnp.bfloat16),
        ),
        in_specs=[vmem] * 3,
        out_specs=(vmem, vmem),
    )(back, target, halo_rows)


def solution(mesh):
    in_specs = (
        P(None, "space", "rep"),
        P(None, "space"),
        P(None, "space", None),
        P(None, "space", None),
        P(None, "space"),
        P(None, "space"),
        P(None, "space", "rep"),
    )
    out_specs = (P(None, "space", "rep"), P(None, "space"))
    return jax.shard_map(body, mesh=mesh, in_specs=in_specs, out_specs=out_specs, check_vma=False)
```

time: 47 us -> 38.1 us (0.81)
  Pallas kernels: 10.6 us -> 4.91 us
  blocking collectives: 15.3 us -> 13.1 us
  local copies, waits for them, and re-layouts: 1.48 us -> 0.73 us
    pallas_call x2, Pallas kernels: 8.2 us -> 2.66 us  [the longest x1 1.51 us: body(): pl.pallas_call(lambda *refs: owner_kernel(plan, *refs), name='owner', com...]
    all_to_all x1, blocking collectives: 15.3 us -> 13.1 us  [swap(): boxed = lax.all_to_all(boxed, ('space', 'rep'), 0, 0, tiled=True)]
    dynamic_slice x1, local copies, waits for them, and re-layouts: 0.75 us -> 0.04 us  [body(): other_part = lax.dynamic_slice_in_dim(desc_rows, (1 - rep) * per, per, 0)]
  transfers between devices with their start and end apart: 2 -> 2, of which waited for: 2 -> 2; matrix products, arithmetic and copies ran while one was open for 2% -> 0% of each run, Pallas kernels for 0% -> 0%
where the time goes in v2:
time: 38.1 us; the launch traced here: 37.8 us
  blocking collectives  13.1 us (34%)
  waiting for transfers between devices  10.7 us (28%)
  starting transfers between devices  7.64 us (20%)
  Pallas kernels  4.91 us (13%)
  local copies, waits for them, and re-layouts  0.73 us (2%)
  between operations  0.69 us (2%)
    all_to_all x1, blocking collectives, swap(): boxed = lax.all_to_all(boxed, ('space', 'rep'), 0, 0, tiled=True)  13.1 us
    all_to_all x1, waiting for transfers between devices, swap(): boxed = lax.all_to_all(boxed, ('space', 'rep'), 0, 0, tiled=True)  9.41 us
    all_to_all x1, starting transfers between devices, swap(): boxed = lax.all_to_all(boxed, ('space', 'rep'), 0, 0, tiled=True)  7.32 us
    pallas_call x1, Pallas kernels, body(): pl.pallas_call(lambda *refs: route_kernel(plan, *refs), name='route', out...  2.25 us
    pallas_call x1, Pallas kernels, body(): pl.pallas_call(lambda *refs: owner_kernel(plan, *refs), name='owner', com...  1.51 us
    ppermute x1, waiting for transfers between devices, body(): other = lax.ppermute(other_part, 'rep', [(0, 1), (1, 0)])  1.28 us
    pallas_call x1, Pallas kernels, body(): pl.pallas_call(lambda *refs: land_kernel(plan, *refs), name='land', compi...  1.15 us
  transfers between devices with their start and end apart: 2, of which 2 were waited for; matrix products, arithmetic and copies ran while one was open for 0% of the time, Pallas kernels for 0%

profile of v2, /device:TPU:0, one launch (start us, length us, event | category | flops | bytes accessed | tf_op | source)
XLA Modules:
  0.0 37.8 jit_solution(2425737048455491297)
XLA Ops:
  0.6 0.0 copy-start.2
  0.6 2.3 %route.1 = (bf16[1088,128]{1,0:T(8,128)(2,1)}, s32[4,128]{1,0:T(4,128)}) custom-call(s32[1]{0:T(128)} %bitcast.refs_0_, s32[4,128]{1,0:T(4,128)} %bitcast.12, s32[4,128]{1,0:T(4,128)} %refs_2_.2, s32[4,16,128]{2,1,0:T(8,128)} %bitcast.11, s32[4,128]{1,0:T(4,128)} %refs_4_.1, s32[4,128]{1,0:T(4,128)} %refs_5_.1, bf16[4,128,128]{2,1,0:T(8,128)(2,1)} %refs_2_.3), custom_call_target="tpu_custom_call" | custom-call | tf_op jit(solution)/shard_map/route/pallas_call | solution.py:298
  2.9 7.3 %all-to-all-start = ((bf16[32,17,2,128]{3,2,1,0:T(2,128)(2,1)}), bf16[32,17,2,128]{3,2,1,0:T(2,128)(2,1)S(1)}, u32[]{:S(2)}, u32[]{:S(2)}) async-start(bf16[32,17,2,128]{3,2,1,0:T(2,128)(2,1)} %bitcast.10), calls=%async_computation | async-start | bytes 557056 | tf_op jit(solution)/shard_map/all_to_all | solution.py:288
  10.2 0.0 copy-done.2
  10.3 0.3 collective-permute-start
  10.6 1.3 %collective-permute-done.refs_3_ = bf16[2,512,128]{2,1,0:T(8,128)(2,1)S(1)} collective-permute-done((bf16[2,512,128]{2,1,0:T(8,128)(2,1)S(1)}, bf16[2,512,128]{2,1,0:T(8,128)(2,1)S(1)}, u32[]{:S(2)}, u32[]{:S(2)}) %collective-permute-start) | collective-permute-done | bytes 262176 | tf_op jit(solution)/shard_map/ppermute | solution.py:292
  11.9 9.4 %all-to-all-done = bf16[32,17,2,128]{3,2,1,0:T(2,128)(2,1)S(1)} async-done(((bf16[32,17,2,128]{3,2,1,0:T(2,128)(2,1)}), bf16[32,17,2,128]{3,2,1,0:T(2,128)(2,1)S(1)}, u32[]{:S(2)}, u32[]{:S(2)}) %all-to-all-start) | async-done | bytes 278560 | tf_op jit(solution)/shard_map/all_to_all | solution.py:288
  21.3 1.5 %owner.1 = bf16[1088,128]{1,0:T(8,128)(2,1)S(1)} custom-call(s32[1]{0:T(128)} %bitcast.refs_0_, bf16[1088,128]{1,0:T(8,128)(2,1)S(1)} %bitcast.7, bf16[2,512,128]{2,1,0:T(8,128)(2,1)S(1)} %get-tuple-element.7.refs_2_, bf16[2,512,128]{2,1,0:T(8,128)(2,1)S(1)} %collective-permute-done.refs_3_), custom_call_target="tpu_custom_call" | custom-call | tf_op jit(solution)/shard_map/owner/pallas_call | solution.py:317
  22.8 0.0 copy-start
  22.8 13.1 %all_to_all.10 = bf16[32,17,2,128]{3,2,1,0:T(2,128)(2,1)S(1)} all-to-all(bf16[32,17,2,128]{3,2,1,0:T(2,128)(2,1)S(1)} %bitcast.9), channel_id=1, replica_groups=mesh['space'=16,'rep'=2] {'space','rep'}, dimensions={0} | all-to-all | bytes 557056 | tf_op jit(solution)/shard_map/all_to_all | solution.py:288
  36.0 0.0 copy-start.1
  36.0 0.0 copy-done
  36.0 0.7 %copy-done.1 = s32[4,128]{1,0:T(4,128)S(1)} copy-done((s32[4,128]{1,0:T(4,128)S(1)}, s32[4,128]{1,0:T(4,128)}, u32[]{:S(2)}) %copy-start.1) | copy-done | bytes 2072
  36.7 1.1 %land.1 = (bf16[4,128,128]{2,1,0:T(8,128)(2,1)}, bf16[4,128]{1,0:T(4,128)(2,1)}) custom-call(bf16[1088,128]{1,0:T(8,128)(2,1)S(1)} %bitcast.8, s32[4,128]{1,0:T(4,128)S(1)} %copy-done.1, bf16[4,128,128]{2,1,0:T(8,128)(2,1)S(1)} %copy-done), custom_call_target="tpu_custom_call" | custom-call | tf_op jit(solution)/shard_map/land/pallas_call | solution.py:326
  (1 shorter events, 0.0 us)
Async XLA Ops:
  0.6 9.6 %copy-start.2 = (bf16[4,512,128]{2,1,0:T(8,128)(2,1)S(1)}, bf16[4,512,128]{2,1,0:T(8,128)(2,1)}, u32[]{:S(2)}) copy-start(bf16[4,512,128]{2,1,0:T(8,128)(2,1)} %param.13) | copy-start | bytes 1572868
  2.9 18.4 %all-to-all-start = ((bf16[32,17,2,128]{3,2,1,0:T(2,128)(2,1)}), bf16[32,17,2,128]{3,2,1,0:T(2,128)(2,1)S(1)}, u32[]{:S(2)}, u32[]{:S(2)}) async-start(bf16[32,17,2,128]{3,2,1,0:T(2,128)(2,1)} %bitcast.10), calls=%async_computation | async-start | bytes 557056 | tf_op jit(solution)/shard_map/all_to_all | solution.py:288
  10.3 1.6 %collective-permute-start = (bf16[2,512,128]{2,1,0:T(8,128)(2,1)S(1)}, bf16[2,512,128]{2,1,0:T(8,128)(2,1)S(1)}, u32[]{:S(2)}, u32[]{:S(2)}) collective-permute-start(bf16[2,512,128]{2,1,0:T(8,128)(2,1)S(1)} %get-tuple-element.6), channel_id=1, source_target_pairs={{0,1},{1,0},{2,3},{3,2},{4,5},{5,4},{6,7},{7,6},{8,9},{9,8},{10,11... | collective-permute-start | bytes 786440 | tf_op jit(solution)/shard_map/ppermute | solution.py:292
  22.8 13.2 %copy-start = (bf16[4,128,128]{2,1,0:T(8,128)(2,1)S(1)}, bf16[4,128,128]{2,1,0:T(8,128)(2,1)}, u32[]{:S(2)}) copy-start(bf16[4,128,128]{2,1,0:T(8,128)(2,1)} %refs_2_.3) | copy-start | bytes 393220
  36.0 0.7 %copy-start.1 = (s32[4,128]{1,0:T(4,128)S(1)}, s32[4,128]{1,0:T(4,128)}, u32[]{:S(2)}) copy-start(s32[4,128]{1,0:T(4,128)} %get-tuple-element.5.refs_1_) | copy-start | bytes 6148

commit v3 on v2

--- a/solution.py
+++ b/solution.py
@@ -57,60 +57,72 @@
         return (peer * self.groups + group) * size
 
 
-def route_kernel(plan, rep_ref, owner_ref, live_ref, cand_ref, span_ref, pick_ref, rows_ref, out_ref, target_ref):
+def route_kernel(plan, rep_ref, *refs):
+    sources, (out_ref, target_ref), held = refs[:6], refs[6:8], refs[8:14]
+    sems = refs[14]
+    copies = [pltpu.make_async_copy(x, y, sems.at[i]) for i, (x, y) in enumerate(zip(sources, held))]
+    for copy in copies:
+        copy.start()
+    owner_ref, live_ref, cand_ref, span_ref, pick_ref, rows_ref = held
     n, h, k = plan.peers, plan.halos, plan.listed
     rep = rep_ref[0]
     upper = onehot(iota((h, h), 0) < iota((h, h), 1))
     peer_ids = iota((n, h), 0)
+    list_ids = iota((k, h), 0)
+    for copy in copies[:-1]:
+        copy.wait()
     owners = [owner_ref[s : s + 1, :] for s in range(plan.snaps)]
     marks = jnp.concatenate([onehot(peer_ids == o) for o in owners], axis=0)
     prefix = dot(marks, upper, 1, 0)
-    list_ids = iota((k, h), 0)
+    puts, says, spreads = [], [], []
+    for s in range(plan.snaps):
+        g, q = s // plan.per, s % plan.per
+        mine = jnp.where(peer_ids == owners[s], prefix[s * n : (s + 1) * n], 0.0)
+        rank = jnp.sum(mine, axis=0, keepdims=True).astype(jnp.int32)
+        live = live_ref[s : s + 1, :] == 1
+        place = q * plan.slots + rank
+        target_ref[s : s + 1, :] = jnp.where(live, owners[s] * LANES + place, -LANES)
+        listing = cand_ref[s]
+        pick = pick_ref[s : s + 1, :]
+        chosen = jnp.sum(jnp.where(list_ids == pick, listing, 0), axis=0, keepdims=True)
+        first = listing[0:1, :]
+        kept = jnp.where(list_ids < span_ref[s : s + 1, :], listing, chosen)
+        kept = jnp.where(list_ids == pick, first, kept)
+        kept = jnp.where(list_ids == 0, chosen, kept)
+        code = jnp.where(kept < plan.half, kept - plan.half, kept - plan.half + 1)
+        code = code.astype(jnp.float32)
+        spot, line = left(place, plan.fit), over(place, plan.fit)
+        spread = jnp.concatenate([jnp.where(spot == b, code, 0.0) for b in range(plan.fit)], axis=0)
+        spreads.append(spread.astype(jnp.bfloat16))
+        tells = live & (over(line, plan.codes) == rep)
+        line = left(line, plan.codes)
+        if plan.aligned:
+            put = iota((n * plan.data, h), 0) == jnp.where(live, owners[s] * plan.data + place, -1)
+            say = iota((n * SUB, h), 0) == jnp.where(tells, owners[s] * SUB + line, -1)
+        else:
+            base = plan.at(owners[s], g, plan.send)
+            ids = iota((n * plan.groups * plan.send, h), 0)
+            put = ids == jnp.where(live, base + place, -1)
+            say = ids == jnp.where(tells, base + plan.data + line, -1)
+        puts.append(onehot(put))
+        says.append(onehot(say))
+    tails = []
+    for g in range(plan.groups):
+        mine = range(g * plan.per, (g + 1) * plan.per)
+        tails.append(sum(dot(says[s], spreads[s], 1, 1) for s in mine))
+    copies[-1].wait()
     whole = None
     for g in range(plan.groups):
-        rows, tail = None, None
-        for q in range(plan.per):
-            s = g * plan.per + q
-            mine = jnp.where(peer_ids == owners[s], prefix[s * n : (s + 1) * n], 0.0)
-            rank = jnp.sum(mine, axis=0, keepdims=True).astype(jnp.int32)
-            live = live_ref[s : s + 1, :] == 1
-            place = q * plan.slots + rank
-            target_ref[s : s + 1, :] = jnp.where(live, owners[s] * LANES + place, -LANES)
-            listing = cand_ref[s]
-            pick = pick_ref[s : s + 1, :]
-            chosen = jnp.sum(jnp.where(list_ids == pick, listing, 0), axis=0, keepdims=True)
-            first = listing[0:1, :]
-            kept = jnp.where(list_ids < span_ref[s : s + 1, :], listing, chosen)
-            kept = jnp.where(list_ids == pick, first, kept)
-            kept = jnp.where(list_ids == 0, chosen, kept)
-            code = jnp.where(kept < plan.half, kept - plan.half, kept - plan.half + 1)
-            code = code.astype(jnp.float32)
-            spot, line = left(place, plan.fit), over(place, plan.fit)
-            spread = jnp.concatenate(
-                [jnp.where(spot == b, code, 0.0) for b in range(plan.fit)], axis=0
-            ).astype(jnp.bfloat16)
-            tells = live & (over(line, plan.codes) == rep)
-            line = left(line, plan.codes)
-            if plan.aligned:
-                put = iota((n * plan.data, h), 0) == jnp.where(live, owners[s] * plan.data + place, -1)
-                say = iota((n * SUB, h), 0) == jnp.where(tells, owners[s] * SUB + line, -1)
-            else:
-                base = plan.at(owners[s], g, plan.send)
-                ids = iota((n * plan.groups * plan.send, h), 0)
-                put = ids == jnp.where(live, base + place, -1)
-                say = ids == jnp.where(tells, base + plan.data + line, -1)
-            part = dot(onehot(put), rows_ref[s], 1, 0)
-            note = dot(onehot(say), spread, 1, 1)
-            rows = part if rows is None else rows + part
-            tail = note if tail is None else tail + note
+        mine = range(g * plan.per, (g + 1) * plan.per)
+        rows = sum(dot(puts[s], rows_ref[s], 1, 0) for s in mine)
         if plan.aligned:
-            rows, tail = rows.astype(jnp.bfloat16), tail.astype(jnp.bfloat16)
+            rows, tail = rows.astype(jnp.bfloat16), tails[g].astype(jnp.bfloat16)
             for p in range(n):
                 base = plan.at(p, g, plan.send)
                 out_ref[base : base + plan.data, :] = rows[p * plan.data : (p + 1) * plan.data]
                 out_ref[base + plan.data : base + plan.send, :] = tail[p * SUB : p * SUB + plan.send - plan.data]
         else:
-            both = rows + tail
+            both = rows + tails[g]
             whole = both if whole is None else whole + both
     if not plan.aligned:
         out_ref[...] = whole.astype(jnp.bfloat16)
@@ -140,7 +152,7 @@
 
 def owner_kernel(plan, rep_ref, got_ref, own_ref, other_ref, out_ref):
     n, t, c, k = plan.peers, plan.total, plan.cands, plan.listed
-    first = rep_ref[0] == 0
+    rep = rep_ref[0]
     scale = 1.0 / math.sqrt(plan.width * plan.groups)
     item = iota((1, t), 1)
     source, slot = over(item, plan.slots), left(item, plan.slots)
@@ -169,9 +181,10 @@
         index = jnp.where(codes < 0, codes + plan.half, codes + plan.half - 1)
         listing.append(jnp.where(codes == 0, -1, index))
 
-    tables = [
-        [jnp.where(first, own_ref[q], other_ref[q]), jnp.where(first, other_ref[q], own_ref[q])] for q in snaps
-    ]
+    tables = []
+    for q in snaps:
+        own, other = own_ref[rep * plan.per + q], other_ref[rep * plan.per + q]
+        tables.append([jnp.where(rep == 0, own, other), jnp.where(rep == 0, other, own)])
     rows = [[rows_in(plan, got_ref, r, q, plan.send) for r in cores] for q in snaps]
     merits = [sum(dot(tables[q][r], rows[q][r], 1, 1) for r in cores) for q in snaps]
 
@@ -281,38 +294,53 @@
     cands, listed = desc_rows.shape[1], cand_index.shape[2]
     plan = Plan(peers, groups, snaps, halos, width, cands, listed)
     rep = lax.axis_index("rep").astype(jnp.int32)
-    per = plan.per
 
     def swap(flat, size):
         boxed = flat.reshape(peers * groups, size // 2, 2, width)
         boxed = lax.all_to_all(boxed, ("space", "rep"), 0, 0, tiled=True)
         return boxed.reshape(peers * groups * size, width)
 
-    other_part = lax.dynamic_slice_in_dim(desc_rows, (1 - rep) * per, per, 0)
-    other = lax.ppermute(other_part, "rep", [(0, 1), (1, 0)])
-    own = lax.dynamic_slice_in_dim(desc_rows, rep * per, per, 0)
+    other = lax.ppermute(desc_rows, "rep", [(0, 1), (1, 0)])
 
     vmem = pl.BlockSpec(memory_space=pltpu.VMEM)
     smem = pl.BlockSpec(memory_space=pltpu.SMEM)
+    hbm = pl.BlockSpec(memory_space=pltpu.HBM)
     small = pltpu.CompilerParams(vmem_limit_bytes=20 << 20)
+    flat = (snaps, halos)
     sent, target = pl.pallas_call(
         lambda *refs: route_kernel(plan, *refs),
         name="route",
+        compiler_params=small,
         out_shape=(
             jax.ShapeDtypeStruct((peers * groups * plan.send, width), jnp.bfloat16),
-            jax.ShapeDtypeStruct((snaps, halos), jnp.int32),
+            jax.ShapeDtypeStruct(flat, jnp.int32),
         ),
-        in_specs=[smem] + [vmem] * 6,
+        in_specs=[smem] + [hbm] * 6,
         out_specs=(vmem, vmem),
+        scratch_shapes=[
+            pltpu.VMEM(flat, jnp.int32),
+            pltpu.VMEM(flat, jnp.int32),
+            pltpu.VMEM((snaps, listed, halos), jnp.int32),
+            pltpu.VMEM(flat, jnp.int32),
+            pltpu.VMEM(flat, jnp.int32),
+            pltpu.VMEM((snaps, halos, width), jnp.bfloat16),
+            pltpu.SemaphoreType.DMA((6,)),
+        ],
     )(
         rep.reshape(1),
-        owner_id.reshape(snaps, halos),
-        unmatched,
-        jnp.swapaxes(cand_index, 1, 2),
-        lengths,
-        choice_index,
-        halo_rows,
+        *(
+            pltpu.with_memory_space_constraint(x, pltpu.HBM)
+            for x in (
+                owner_id.reshape(flat),
+                unmatched,
+                jnp.swapaxes(cand_index, 1, 2),
+                lengths,
+                choice_index,
+                halo_rows,
+            )
+        ),
     )
+    sent, other = lax.optimization_barrier((sent, other))
     got = swap(sent, plan.send)
     reply = pl.pallas_call(
         lambda *refs: owner_kernel(plan, *refs),
@@ -321,7 +349,7 @@
         out_shape=jax.ShapeDtypeStruct((peers * groups * plan.back, width), jnp.bfloat16),
         in_specs=[smem, vmem, vmem, vmem],
         out_specs=vmem,
-    )(rep.reshape(1), got, own, other)
+    )(rep.reshape(1), got, desc_rows, other)
     back = swap(reply, plan.back)
     return pl.pallas_call(
         lambda *refs: land_kernel(plan, *refs),

time: 38.1 us -> 37 us (0.971)
  blocking collectives: 13.1 us -> 31.2 us
  waiting for transfers between devices: 10.7 us -> 0.12 us
  starting transfers between devices: 7.64 us -> 0.56 us
  local copies, waits for them, and re-layouts: 0.73 us -> 0.01 us
  Pallas kernels: 4.91 us -> 4.29 us
    all_to_all x1 -> x2, blocking collectives: 13.1 us -> 31.2 us  [swap(): boxed = lax.all_to_all(boxed, ('space', 'rep'), 0, 0, tiled=True)]
    all_to_all x1 -> x0, waiting for transfers between devices: 9.41 us -> none  [swap(): boxed = lax.all_to_all(boxed, ('space', 'rep'), 0, 0, tiled=True)]
    all_to_all x1 -> x0, starting transfers between devices: 7.32 us -> none  [swap(): boxed = lax.all_to_all(boxed, ('space', 'rep'), 0, 0, tiled=True)]
    ppermute x1, waiting for transfers between devices: 1.28 us -> 0.12 us  [body(): other = lax.ppermute(desc_rows, 'rep', [(0, 1), (1, 0)])]
    unnamed x6 -> x4, local copies, waits for them, and re-layouts: 0.69 us -> 0.01 us
    pallas_call x1, Pallas kernels: 2.25 us -> 1.62 us  [body(): pl.pallas_call(lambda *refs: route_kernel(plan, *refs), name='route', com...]
  transfers between devices with their start and end apart: 2 -> 1, of which waited for: 2 -> 1; matrix products, arithmetic and copies ran while one was open for 0% -> 0% of each run, Pallas kernels for 0% -> 4%
where the time goes in v3:
time: 37 us; the launch traced here: 36.8 us
  blocking collectives  31.2 us (84%)
  Pallas kernels  4.29 us (12%)
  between operations  0.67 us (2%)
  starting transfers between devices  0.56 us (2%)
    all_to_all x2, blocking collectives, swap(): boxed = lax.all_to_all(boxed, ('space', 'rep'), 0, 0, tiled=True)  31.2 us
    pallas_call x1, Pallas kernels, body(): pl.pallas_call(lambda *refs: route_kernel(plan, *refs), name='route', com...  1.62 us
    pallas_call x1, Pallas kernels, body(): pl.pallas_call(lambda *refs: owner_kernel(plan, *refs), name='owner', com...  1.53 us
    pallas_call x1, Pallas kernels, body(): pl.pallas_call(lambda *refs: land_kernel(plan, *refs), name='land', compi...  1.15 us
  transfers between devices with their start and end apart: 1, of which 1 were waited for; matrix products, arithmetic and copies ran while one was open for 0% of the time, Pallas kernels for 4%

profile of v3, /device:TPU:0, one launch (start us, length us, event | category | flops | bytes accessed | tf_op | source)
XLA Modules:
  0.0 36.8 jit_solution(8544765239225102924)
XLA Ops:
  0.6 0.0 copy-start.1
  0.6 0.6 %collective-permute-start = (bf16[4,512,128]{2,1,0:T(8,128)(2,1)}, bf16[4,512,128]{2,1,0:T(8,128)(2,1)S(1)}, u32[]{:S(2)}, u32[]{:S(2)}) collective-permute-start(bf16[4,512,128]{2,1,0:T(8,128)(2,1)} %refs_2_.4), channel_id=1, source_target_pairs={{0,1},{1,0},{2,3},{3,2},{4,5},{5,4},{6,7},{7,6},{8,9},{9,8},{10,11... | collective-permute-start | bytes 1572872 | tf_op jit(solution)/shard_map/ppermute | solution.py:303
  1.2 1.6 %route.1 = (bf16[1088,128]{1,0:T(8,128)(2,1)S(1)}, s32[4,128]{1,0:T(4,128)S(1)}) custom-call(s32[1]{0:T(128)} %bitcast.refs_0_, s32[4,128]{1,0:T(4,128)} %bitcast.12, s32[4,128]{1,0:T(4,128)} %refs_2_.3, s32[4,16,128]{2,1,0:T(8,128)} %bitcast.11, s32[4,128]{1,0:T(4,128)} %refs_4_.1, s32[4,128]{1,0:T(4,128)} %refs_5_.1, bf16[4,128,128]{2,1,0:T(8,128)(2,1)} %refs_2_.5), custom_call_target="tpu_custom_call" | custom-call | tf_op jit(solution)/shard_map/route/pallas_call | solution.py:310
  2.8 0.1 collective-permute-done.refs_3_
  2.9 18.1 %all_to_all.10 = bf16[32,17,2,128]{3,2,1,0:T(2,128)(2,1)S(1)} all-to-all(bf16[32,17,2,128]{3,2,1,0:T(2,128)(2,1)S(1)} %bitcast.10), channel_id=1, replica_groups=mesh['space'=16,'rep'=2] {'space','rep'}, dimensions={0} | all-to-all | bytes 557056 | tf_op jit(solution)/shard_map/all_to_all | solution.py:300
  21.0 0.0 copy-done.1
  21.0 1.5 %owner.1 = bf16[1088,128]{1,0:T(8,128)(2,1)S(1)} custom-call(s32[1]{0:T(128)} %bitcast.refs_0_, bf16[1088,128]{1,0:T(8,128)(2,1)S(1)} %bitcast.8, bf16[4,512,128]{2,1,0:T(8,128)(2,1)S(1)} %copy-done.1, bf16[4,512,128]{2,1,0:T(8,128)(2,1)S(1)} %collective-permute-done.refs_3_), custom_call_target="tpu_custom_call" | custom-call | tf_op jit(solution)/shard_map/owner/pallas_call | solution.py:345
  22.6 0.0 copy-start
  22.6 13.1 %all_to_all.11 = bf16[32,17,2,128]{3,2,1,0:T(2,128)(2,1)S(1)} all-to-all(bf16[32,17,2,128]{3,2,1,0:T(2,128)(2,1)S(1)} %bitcast.9), channel_id=1, replica_groups=mesh['space'=16,'rep'=2] {'space','rep'}, dimensions={0} | all-to-all | bytes 557056 | tf_op jit(solution)/shard_map/all_to_all | solution.py:300
  35.7 0.0 copy-done
  35.7 1.1 %land.1 = (bf16[4,128,128]{2,1,0:T(8,128)(2,1)}, bf16[4,128]{1,0:T(4,128)(2,1)}) custom-call(bf16[1088,128]{1,0:T(8,128)(2,1)S(1)} %bitcast.7, s32[4,128]{1,0:T(4,128)S(1)} %get-tuple-element.9.refs_1_, bf16[4,128,128]{2,1,0:T(8,128)(2,1)S(1)} %copy-done), custom_call_target="tpu_custom_call" | custom-call | tf_op jit(solution)/shard_map/land/pallas_call | solution.py:354
Async XLA Ops:
  0.6 20.4 %copy-start.1 = (bf16[4,512,128]{2,1,0:T(8,128)(2,1)S(1)}, bf16[4,512,128]{2,1,0:T(8,128)(2,1)}, u32[]{:S(2)}) copy-start(bf16[4,512,128]{2,1,0:T(8,128)(2,1)} %refs_2_.4) | copy-start | bytes 1572868
  0.6 2.3 %collective-permute-start = (bf16[4,512,128]{2,1,0:T(8,128)(2,1)}, bf16[4,512,128]{2,1,0:T(8,128)(2,1)S(1)}, u32[]{:S(2)}, u32[]{:S(2)}) collective-permute-start(bf16[4,512,128]{2,1,0:T(8,128)(2,1)} %refs_2_.4), channel_id=1, source_target_pairs={{0,1},{1,0},{2,3},{3,2},{4,5},{5,4},{6,7},{7,6},{8,9},{9,8},{10,11... | collective-permute-start | bytes 1572872 | tf_op jit(solution)/shard_map/ppermute | solution.py:303
  22.6 13.1 %copy-start = (bf16[4,128,128]{2,1,0:T(8,128)(2,1)S(1)}, bf16[4,128,128]{2,1,0:T(8,128)(2,1)}, u32[]{:S(2)}) copy-start(bf16[4,128,128]{2,1,0:T(8,128)(2,1)} %refs_2_.5) | copy-start | bytes 393220

commit v4 on v3

--- a/solution.py
+++ b/solution.py
@@ -25,8 +25,9 @@
     return x & (m - 1) if m & (m - 1) == 0 else x % m
 
 
-def onehot(mask):
-    return jnp.where(mask, 1.0, 0.0).astype(jnp.bfloat16)
+def hot(shape, axis, spot):
+    mask = lax.broadcasted_iota(jnp.int16, shape, axis) == spot.astype(jnp.int16)
+    return jnp.where(mask, jnp.bfloat16(1), jnp.bfloat16(0))
 
 
 def dot(a, b, ca, cb):
@@ -66,13 +67,14 @@
     owner_ref, live_ref, cand_ref, span_ref, pick_ref, rows_ref = held
     n, h, k = plan.peers, plan.halos, plan.listed
     rep = rep_ref[0]
-    upper = onehot(iota((h, h), 0) < iota((h, h), 1))
+    upper = iota((h, h), 0) < iota((h, h), 1)
+    upper = jnp.where(upper, 1.0, 0.0).astype(jnp.bfloat16)
     peer_ids = iota((n, h), 0)
     list_ids = iota((k, h), 0)
     for copy in copies[:-1]:
         copy.wait()
     owners = [owner_ref[s : s + 1, :] for s in range(plan.snaps)]
-    marks = jnp.concatenate([onehot(peer_ids == o) for o in owners], axis=0)
+    marks = jnp.concatenate([hot((n, h), 0, o) for o in owners], axis=0)
     prefix = dot(marks, upper, 1, 0)
     puts, says, spreads = [], [], []
     for s in range(plan.snaps):
@@ -90,31 +92,34 @@
         kept = jnp.where(list_ids == pick, first, kept)
         kept = jnp.where(list_ids == 0, chosen, kept)
         code = jnp.where(kept < plan.half, kept - plan.half, kept - plan.half + 1)
-        code = code.astype(jnp.float32)
-        spot, line = left(place, plan.fit), over(place, plan.fit)
-        spread = jnp.concatenate([jnp.where(spot == b, code, 0.0) for b in range(plan.fit)], axis=0)
-        spreads.append(spread.astype(jnp.bfloat16))
+        code = code.astype(jnp.float32).astype(jnp.bfloat16)
+        spot, line = left(place, plan.fit).astype(jnp.int16), over(place, plan.fit)
+        spreads.append(
+            jnp.concatenate(
+                [jnp.where(jnp.broadcast_to(spot, (k, h)) == b, code, jnp.bfloat16(0)) for b in range(plan.fit)],
+                axis=0,
+            )
+        )
         tells = live & (over(line, plan.codes) == rep)
         line = left(line, plan.codes)
         if plan.aligned:
-            put = iota((n * plan.data, h), 0) == jnp.where(live, owners[s] * plan.data + place, -1)
-            say = iota((n * SUB, h), 0) == jnp.where(tells, owners[s] * SUB + line, -1)
+            puts.append(hot((n * plan.data, h), 0, jnp.where(live, owners[s] * plan.data + place, -1)))
+            says.append(hot((n * SUB, h), 0, jnp.where(tells, owners[s] * SUB + line, -1)))
         else:
             base = plan.at(owners[s], g, plan.send)
-            ids = iota((n * plan.groups * plan.send, h), 0)
-            put = ids == jnp.where(live, base + place, -1)
-            say = ids == jnp.where(tells, base + plan.data + line, -1)
-        puts.append(onehot(put))
-        says.append(onehot(say))
-    tails = []
-    for g in range(plan.groups):
-        mine = range(g * plan.per, (g + 1) * plan.per)
-        tails.append(sum(dot(says[s], spreads[s], 1, 1) for s in mine))
+            shape = (n * plan.groups * plan.send, h)
+            puts.append(hot(shape, 0, jnp.where(live, base + place, -1)))
+            says.append(hot(shape, 0, jnp.where(tells, base + plan.data + line, -1)))
+
+    def joined(parts, g, axis):
+        return jnp.concatenate(parts[g * plan.per : (g + 1) * plan.per], axis=axis)
+
+    tails = [dot(joined(says, g, 1), joined(spreads, g, 1), 1, 1) for g in range(plan.groups)]
     copies[-1].wait()
     whole = None
     for g in range(plan.groups):
-        mine = range(g * plan.per, (g + 1) * plan.per)
-        rows = sum(dot(puts[s], rows_ref[s], 1, 0) for s in mine)
+        held_rows = rows_ref[g * plan.per : (g + 1) * plan.per].reshape(plan.per * h, plan.width)
+        rows = dot(joined(puts, g, 1), held_rows, 1, 0)
         if plan.aligned:
             rows, tail = rows.astype(jnp.bfloat16), tails[g].astype(jnp.bfloat16)
             for p in range(n):
@@ -136,10 +141,10 @@
     if plan.aligned:
         starts = [plan.at(p, group, size) + q * plan.slots for p in range(plan.peers)]
         return jnp.concatenate([ref[a : a + plan.slots, :] for a in starts], axis=0)
-    shape = (plan.total, plan.peers * plan.groups * size)
-    item = iota(shape, 0)
+    item = iota((plan.total, 1), 0)
     spot = plan.at(over(item, plan.slots), group, size) + q * plan.slots + left(item, plan.slots)
-    return dot(onehot(iota(shape, 1) == spot), ref[...], 1, 0).astype(jnp.bfloat16)
+    take = hot((plan.total, plan.peers * plan.groups * size), 1, spot)
+    return dot(take, ref[...], 1, 0).astype(jnp.bfloat16)
 
 
 def tail_in(plan, ref, group, size):
@@ -158,6 +163,13 @@
     source, slot = over(item, plan.slots), left(item, plan.slots)
     snaps, cores = range(plan.per), range(plan.groups)
     ends = [tail_in(plan, got_ref, r, plan.send) for r in cores]
+
+    tables, rows, merits = [], [], []
+    for q in snaps:
+        own, other = own_ref[rep * plan.per + q], other_ref[rep * plan.per + q]
+        pair = [jnp.where(rep == 0, own, other), jnp.where(rep == 0, other, own)]
+        tables.append(jnp.concatenate(pair, axis=1))
+        rows.append(jnp.concatenate([rows_in(plan, got_ref, r, q, plan.send) for r in cores], axis=1))
 
     listing = []
     for q in snaps:
@@ -171,29 +183,24 @@
             if q * plan.slots // plan.fit // plan.codes > r:
                 continue
             told = jnp.where(over(line, plan.codes) == r, row(source) + left(line, plan.codes), -1)
-            piece = dot(value, onehot(iota((value.shape[0], t), 0) == told), 0, 0)
+            piece = dot(value, hot((value.shape[0], t), 0, told), 0, 0)
             wide = piece if wide is None else wide + piece
-        codes = None
-        for b in range(plan.fit):
-            piece = jnp.where(spot == b, wide[b * k : (b + 1) * k], 0.0)
-            codes = piece if codes is None else codes + piece
+        codes = wide[0:k]
+        for b in range(1, plan.fit):
+            codes = jnp.where(spot == b, wide[b * k : (b + 1) * k], codes)
         codes = codes.astype(jnp.int32)
         index = jnp.where(codes < 0, codes + plan.half, codes + plan.half - 1)
         listing.append(jnp.where(codes == 0, -1, index))
-
-    tables = []
-    for q in snaps:
-        own, other = own_ref[rep * plan.per + q], other_ref[rep * plan.per + q]
-        tables.append([jnp.where(rep == 0, own, other), jnp.where(rep == 0, other, own)])
-    rows = [[rows_in(plan, got_ref, r, q, plan.send) for r in cores] for q in snaps]
-    merits = [sum(dot(tables[q][r], rows[q][r], 1, 1) for r in cores) for q in snaps]
+        merits.append(dot(tables[q], rows[q], 1, 1))
 
     words = c // WORD
     word_ids = iota((words, t), 0)
-    bits = jnp.left_shift(jnp.int32(1), iota((WORD, t), 0))
+    line_ids = iota((WORD, t), 0)
+    bits = jnp.left_shift(jnp.int32(1), line_ids)
+    filler = jnp.zeros((SUB - plan.per, t), jnp.float32)
     heads = [listing[q][0:1, :].astype(jnp.float32) for q in snaps]
-    heads = jnp.transpose(jnp.concatenate(heads + [jnp.zeros((SUB - plan.per, t), jnp.float32)], axis=0))
-    heads = heads.astype(jnp.int32)
+    heads = jnp.transpose(jnp.concatenate(heads + [filler], axis=0)).astype(jnp.int32)
+    descs = [dot(hot((t, c), 1, heads[:, q : q + 1]), tables[q], 1, 0) for q in snaps]
     bests, shares = [], []
     for q in snaps:
         index = listing[q]
@@ -201,91 +208,85 @@
         sets = jnp.zeros((words, t), jnp.int32)
         for j in range(k):
             sets = sets | jnp.where(high[j : j + 1, :] == word_ids, bit[j : j + 1, :], 0)
-        parts = []
+        head = index[0:1, :]
+        best = jnp.full((WORD, t), NEG, jnp.float32)
+        picked = jnp.zeros((WORD, t), jnp.float32)
+        rival = jnp.zeros((WORD, t), jnp.float32)
         for w in range(words):
+            merit = merits[q][w * WORD : (w + 1) * WORD]
             member = (sets[w : w + 1, :] & bits) != 0
-            parts.append(jnp.where(member, merits[q][w * WORD : (w + 1) * WORD], NEG))
-        listed = jnp.concatenate(parts, axis=0)
-        bests.append(jnp.max(listed, axis=0, keepdims=True) * scale)
-        top = jnp.max(listed, axis=1, keepdims=True)
-        chosen = iota((c, t), 0) == index[0:1, :]
-        picked = jnp.sum(jnp.where(chosen, merits[q], 0.0), axis=0, keepdims=True) * scale
-        rival = jnp.sum(jnp.where(chosen, top, 0.0), axis=0, keepdims=True) * scale
-        mine, claim = soft(picked), soft(rival)
+            listed = jnp.where(member, merit, NEG)
+            best = jnp.maximum(best, listed)
+            top = jnp.max(listed, axis=1, keepdims=True)
+            chosen = line_ids == head - w * WORD
+            picked = jnp.where(chosen, merit, picked)
+            rival = jnp.where(chosen, top, rival)
+        bests.append((jnp.max(best, axis=0, keepdims=True) * scale).astype(jnp.bfloat16))
+        mine = soft(jnp.sum(picked, axis=0, keepdims=True) * scale)
+        claim = soft(jnp.sum(rival, axis=0, keepdims=True) * scale)
         shares.append(mine / (mine + claim))
-    shares = jnp.transpose(jnp.concatenate(shares + [jnp.zeros((SUB - plan.per, t), jnp.float32)], axis=0))
+    shares = jnp.transpose(jnp.concatenate(shares + [filler], axis=0))
 
     blends = []
     for q in snaps:
-        select = onehot(iota((t, c), 1) == heads[:, q : q + 1])
         share = shares[:, q : q + 1]
-        pair = []
-        for r in cores:
-            desc = dot(select, tables[q][r], 1, 0)
-            pair.append(((1.0 - share) * rows[q][r].astype(jnp.float32) + share * desc).astype(jnp.bfloat16))
-        blends.append(pair)
-
-    tail = None
-    lane = iota((t, LANES), 1)
-    for q in snaps:
-        if plan.aligned:
-            shape = (n * SUB, t)
-            home = source * SUB
-        else:
-            shape = (n * plan.back, t)
-            home = source * plan.back + plan.data
-        line = jnp.where(iota(shape, 0) == home, jnp.maximum(bests[q], NEG), 0.0).astype(jnp.bfloat16)
-        piece = dot(line, onehot(lane == q * plan.slots + left(iota((t, LANES), 0), plan.slots)), 1, 0)
-        tail = piece if tail is None else tail + piece
+        blend = (1.0 - share) * rows[q].astype(jnp.float32) + share * descs[q]
+        blends.append(blend.astype(jnp.bfloat16))
+
+    tall = SUB if plan.aligned else plan.back
+    home = source * tall + (0 if plan.aligned else plan.data)
+    here = lax.broadcasted_iota(jnp.int16, (n * tall, t), 0) == home.astype(jnp.int16)
+    lines = [jnp.where(here, bests[q], jnp.bfloat16(0)) for q in snaps]
+    slot_of = left(iota((t, 1), 0), plan.slots)
+    lanes = [hot((t, LANES), 1, q * plan.slots + slot_of) for q in snaps]
+    tail = dot(jnp.concatenate(lines, axis=1), jnp.concatenate(lanes, axis=0), 1, 0).astype(jnp.bfloat16)
+    width = plan.width
     if plan.aligned:
-        tail = tail.astype(jnp.bfloat16)
         for r in cores:
             for p in range(n):
                 base = plan.at(p, r, plan.back)
                 for q in snaps:
                     a = base + q * plan.slots
-                    out_ref[a : a + plan.slots, :] = blends[q][r][p * plan.slots : (p + 1) * plan.slots]
+                    out_ref[a : a + plan.slots, :] = blends[q][
+                        p * plan.slots : (p + 1) * plan.slots, r * width : (r + 1) * width
+                    ]
                 out_ref[base + plan.data : base + plan.back, :] = tail[p * SUB : p * SUB + plan.back - plan.data]
         return
-    shape = (n * plan.groups * plan.back, t)
-    item = iota(shape, 1)
-    peer, slot = over(item, plan.slots), left(item, plan.slots)
-    shape_tail = (n * plan.groups * plan.back, n * plan.back)
-    row, col = iota(shape_tail, 0), iota(shape_tail, 1)
-    peer_of, line_of = col // plan.back, col % plan.back
+    height = n * plan.groups * plan.back
+    col = iota((1, n * tall), 1)
     full = None
     for r in cores:
-        copy = onehot(row == plan.at(peer_of, r, plan.back) + line_of)
-        piece = dot(copy, tail.astype(jnp.bfloat16), 1, 0)
+        piece = dot(hot((height, n * tall), 0, plan.at(col // tall, r, tall) + col % tall), tail, 1, 0)
         for q in snaps:
-            put = onehot(iota(shape, 0) == plan.at(peer, r, plan.back) + q * plan.slots + slot)
-            piece = piece + dot(put, blends[q][r], 1, 0)
+            put = hot((height, t), 0, plan.at(source, r, plan.back) + q * plan.slots + slot)
+            piece = piece + dot(put, blends[q][:, r * width : (r + 1) * width], 1, 0)
         full = piece if full is None else full + piece
     out_ref[...] = full.astype(jnp.bfloat16)
 
 
 def land_kernel(plan, back_ref, target_ref, rows_ref, out_ref, best_ref):
-    h = plan.halos
+    h, t = plan.halos, plan.total
     target = target_ref[...]
     column = jnp.transpose(target)
-    same = iota((h, h), 0) == iota((h, h), 1)
+    own_row = iota((h, 1), 0) + t
     for g in range(plan.groups):
         tail, row = tail_in(plan, back_ref, g, plan.back)
+        pulls = []
         for q in range(plan.per):
             s = g * plan.per + q
             spot = column[:, s : s + 1]
             owner, slot = spot >> 7, (spot & (LANES - 1)) - q * plan.slots
-            rows = rows_in(plan, back_ref, g, q, plan.back)
-            where_from = jnp.where(spot >= 0, owner * plan.slots + slot, -1)
-            take = onehot(iota((h, plan.total), 1) == where_from)
-            keep = onehot(same & (spot < 0))
-            out_ref[s] = (dot(take, rows, 1, 0) + dot(keep, rows_ref[s], 1, 0)).astype(jnp.bfloat16)
+            spot = jnp.where(spot >= 0, owner * plan.slots + slot, own_row)
+            rows = jnp.concatenate([rows_in(plan, back_ref, g, q, plan.back), rows_ref[s]], axis=0)
+            out_ref[s] = dot(hot((h, t + h), 1, spot), rows, 1, 0).astype(jnp.bfloat16)
             spot = target[s : s + 1, :]
-            owner, place = spot >> 7, spot & (LANES - 1)
-            pull = onehot(iota((tail.shape[0], h), 0) == jnp.where(spot >= 0, row(owner), -1))
-            grid = dot(tail, pull, 0, 0)
-            grid = jnp.where(iota((LANES, h), 0) == place, grid, 0.0)
-            best_ref[s : s + 1, :] = jnp.sum(grid, axis=0, keepdims=True).astype(jnp.bfloat16)
+            pulls.append(hot((tail.shape[0], h), 0, jnp.where(spot >= 0, row(spot >> 7), -1)))
+        grid = dot(tail, jnp.concatenate(pulls, axis=1), 0, 0)
+        for q in range(plan.per):
+            s = g * plan.per + q
+            place = target[s : s + 1, :] & (LANES - 1)
+            mine = jnp.where(iota((LANES, h), 0) == place, grid[:, q * h : (q + 1) * h], 0.0)
+            best_ref[s : s + 1, :] = jnp.sum(mine, axis=0, keepdims=True).astype(jnp.bfloat16)
 
 
 def body(halo_rows, unmatched, owner_id, cand_index, lengths, choice_index, desc_rows):

time: 37 us -> 36.8 us (level)
  no operation moved by 1% of the time
where the time goes in v4:
time: 36.8 us; the launch traced here: 36.6 us
  blocking collectives  31.2 us (85%)
  Pallas kernels  3.98 us (11%)
  between operations  0.67 us (2%)
  starting transfers between devices  0.56 us (2%)
    all_to_all x2, blocking collectives, swap(): boxed = lax.all_to_all(boxed, ('space', 'rep'), 0, 0, tiled=True)  31.2 us
    pallas_call x1, Pallas kernels, body(): pl.pallas_call(lambda *refs: route_kernel(plan, *refs), name='route', com...  1.51 us
    pallas_call x1, Pallas kernels, body(): pl.pallas_call(lambda *refs: owner_kernel(plan, *refs), name='owner', com...  1.39 us
    pallas_call x1, Pallas kernels, body(): pl.pallas_call(lambda *refs: land_kernel(plan, *refs), name='land', compi...  1.08 us
  transfers between devices with their start and end apart: 1, of which 1 were waited for; matrix products, arithmetic and copies ran while one was open for 0% of the time, Pallas kernels for 4%

profile of v4, /device:TPU:0, one launch (start us, length us, event | category | flops | bytes accessed | tf_op | source)
XLA Modules:
  0.0 36.6 jit_solution(17179053171671061827)
XLA Ops:
  0.6 0.0 copy-start.1
  0.6 0.6 %collective-permute-start = (bf16[4,512,128]{2,1,0:T(8,128)(2,1)}, bf16[4,512,128]{2,1,0:T(8,128)(2,1)S(1)}, u32[]{:S(2)}, u32[]{:S(2)}) collective-permute-start(bf16[4,512,128]{2,1,0:T(8,128)(2,1)} %refs_2_.4), channel_id=1, source_target_pairs={{0,1},{1,0},{2,3},{3,2},{4,5},{5,4},{6,7},{7,6},{8,9},{9,8},{10,11... | collective-permute-start | bytes 1572872 | tf_op jit(solution)/shard_map/ppermute | solution.py:304
  1.2 1.5 %route.1 = (bf16[1088,128]{1,0:T(8,128)(2,1)S(1)}, s32[4,128]{1,0:T(4,128)S(1)}) custom-call(s32[1]{0:T(128)} %bitcast.refs_0_, s32[4,128]{1,0:T(4,128)} %bitcast.12, s32[4,128]{1,0:T(4,128)} %refs_2_.3, s32[4,16,128]{2,1,0:T(8,128)} %bitcast.11, s32[4,128]{1,0:T(4,128)} %refs_4_.1, s32[4,128]{1,0:T(4,128)} %refs_5_.1, bf16[4,128,128]{2,1,0:T(8,128)(2,1)} %refs_2_.5), custom_call_target="tpu_custom_call" | custom-call | tf_op jit(solution)/shard_map/route/pallas_call | solution.py:311
  2.7 0.2 collective-permute-done.refs_3_
  2.9 18.1 %all_to_all.10 = bf16[32,17,2,128]{3,2,1,0:T(2,128)(2,1)S(1)} all-to-all(bf16[32,17,2,128]{3,2,1,0:T(2,128)(2,1)S(1)} %bitcast.10), channel_id=1, replica_groups=mesh['space'=16,'rep'=2] {'space','rep'}, dimensions={0} | all-to-all | bytes 557056 | tf_op jit(solution)/shard_map/all_to_all | solution.py:301
  21.0 0.0 copy-done.1
  21.0 1.4 %owner.1 = bf16[1088,128]{1,0:T(8,128)(2,1)S(1)} custom-call(s32[1]{0:T(128)} %bitcast.refs_0_, bf16[1088,128]{1,0:T(8,128)(2,1)S(1)} %bitcast.8, bf16[4,512,128]{2,1,0:T(8,128)(2,1)S(1)} %copy-done.1, bf16[4,512,128]{2,1,0:T(8,128)(2,1)S(1)} %collective-permute-done.refs_3_), custom_call_target="tpu_custom_call" | custom-call | tf_op jit(solution)/shard_map/owner/pallas_call | solution.py:346
  22.4 0.0 copy-start
  22.4 13.1 %all_to_all.11 = bf16[32,17,2,128]{3,2,1,0:T(2,128)(2,1)S(1)} all-to-all(bf16[32,17,2,128]{3,2,1,0:T(2,128)(2,1)S(1)} %bitcast.9), channel_id=1, replica_groups=mesh['space'=16,'rep'=2] {'space','rep'}, dimensions={0} | all-to-all | bytes 557056 | tf_op jit(solution)/shard_map/all_to_all | solution.py:301
  35.6 0.0 copy-done
  35.6 1.1 %land.1 = (bf16[4,128,128]{2,1,0:T(8,128)(2,1)}, bf16[4,128]{1,0:T(4,128)(2,1)}) custom-call(bf16[1088,128]{1,0:T(8,128)(2,1)S(1)} %bitcast.7, s32[4,128]{1,0:T(4,128)S(1)} %get-tuple-element.9.refs_1_, bf16[4,128,128]{2,1,0:T(8,128)(2,1)S(1)} %copy-done), custom_call_target="tpu_custom_call" | custom-call | tf_op jit(solution)/shard_map/land/pallas_call | solution.py:355
Async XLA Ops:
  0.6 20.4 %copy-start.1 = (bf16[4,512,128]{2,1,0:T(8,128)(2,1)S(1)}, bf16[4,512,128]{2,1,0:T(8,128)(2,1)}, u32[]{:S(2)}) copy-start(bf16[4,512,128]{2,1,0:T(8,128)(2,1)} %refs_2_.4) | copy-start | bytes 1572868
  0.6 2.3 %collective-permute-start = (bf16[4,512,128]{2,1,0:T(8,128)(2,1)}, bf16[4,512,128]{2,1,0:T(8,128)(2,1)S(1)}, u32[]{:S(2)}, u32[]{:S(2)}) collective-permute-start(bf16[4,512,128]{2,1,0:T(8,128)(2,1)} %refs_2_.4), channel_id=1, source_target_pairs={{0,1},{1,0},{2,3},{3,2},{4,5},{5,4},{6,7},{7,6},{8,9},{9,8},{10,11... | collective-permute-start | bytes 1572872 | tf_op jit(solution)/shard_map/ppermute | solution.py:304
  22.4 13.1 %copy-start = (bf16[4,128,128]{2,1,0:T(8,128)(2,1)S(1)}, bf16[4,128,128]{2,1,0:T(8,128)(2,1)}, u32[]{:S(2)}) copy-start(bf16[4,128,128]{2,1,0:T(8,128)(2,1)} %refs_2_.5) | copy-start | bytes 393220

commit v5 on v4

--- a/solution.py
+++ b/solution.py
@@ -155,7 +155,7 @@
     return ref[...], (lambda p: plan.at(p, group, size) + plan.data)
 
 
-def owner_kernel(plan, rep_ref, got_ref, own_ref, other_ref, out_ref):
+def owner_kernel(plan, rep_ref, got_ref, own_ref, other_ref, peek_ref, out_ref):
     n, t, c, k = plan.peers, plan.total, plan.cands, plan.listed
     rep = rep_ref[0]
     scale = 1.0 / math.sqrt(plan.width * plan.groups)
@@ -307,6 +307,7 @@
     smem = pl.BlockSpec(memory_space=pltpu.SMEM)
     hbm = pl.BlockSpec(memory_space=pltpu.HBM)
     small = pltpu.CompilerParams(vmem_limit_bytes=20 << 20)
+    packed = pltpu.CompilerParams(vmem_limit_bytes=20 << 20)
     flat = (snaps, halos)
     sent, target = pl.pallas_call(
         lambda *refs: route_kernel(plan, *refs),
@@ -341,21 +342,21 @@
             )
         ),
     )
-    sent, other = lax.optimization_barrier((sent, other))
     got = swap(sent, plan.send)
+    peek = got[0:SUB] * jnp.bfloat16(2)
     reply = pl.pallas_call(
         lambda *refs: owner_kernel(plan, *refs),
         name="owner",
-        compiler_params=small,
+        compiler_params=packed,
         out_shape=jax.ShapeDtypeStruct((peers * groups * plan.back, width), jnp.bfloat16),
-        in_specs=[smem, vmem, vmem, vmem],
+        in_specs=[smem, vmem, vmem, vmem, vmem],
         out_specs=vmem,
-    )(rep.reshape(1), got, desc_rows, other)
+    )(rep.reshape(1), got, desc_rows, other, peek)
     back = swap(reply, plan.back)
     return pl.pallas_call(
         lambda *refs: land_kernel(plan, *refs),
         name="land",
-        compiler_params=small,
+        compiler_params=packed,
         out_shape=(
             jax.ShapeDtypeStruct((snaps, halos, width), jnp.bfloat16),
             jax.ShapeDtypeStruct((snaps, halos), jnp.bfloat16),
@@ -376,4 +377,5 @@
         P(None, "space", "rep"),
     )
     out_specs = (P(None, "space", "rep"), P(None, "space"))
+
     return jax.shard_map(body, mesh=mesh, in_specs=in_specs, out_specs=out_specs, check_vma=False)

time: 36.8 us -> 37.2 us (1.011)
  blocking collectives: 31.2 us -> 13.1 us
  waiting for transfers between devices: 0.23 us -> 10.7 us
  starting transfers between devices: 0.56 us -> 7.65 us
  Pallas kernels: 3.98 us -> 4.73 us
    all_to_all x2 -> x1, blocking collectives: 31.2 us -> 13.1 us  [swap(): boxed = lax.all_to_all(boxed, ('space', 'rep'), 0, 0, tiled=True)]
    all_to_all x0 -> x1, waiting for transfers between devices: none -> 10.7 us  [swap(): boxed = lax.all_to_all(boxed, ('space', 'rep'), 0, 0, tiled=True)]
    all_to_all x0 -> x1, starting transfers between devices: none -> 7.33 us  [swap(): boxed = lax.all_to_all(boxed, ('space', 'rep'), 0, 0, tiled=True)]
    pallas_call x1, Pallas kernels: 1.51 us -> 2.26 us  [body(): pl.pallas_call(lambda *refs: route_kernel(plan, *refs), name='route', com...]
  transfers between devices with their start and end apart: 1 -> 2, of which waited for: 1 -> 1; matrix products, arithmetic and copies ran while one was open for 0% -> 0% of each run, Pallas kernels for 4% -> 0%
where the time goes in v5:
time: 37.2 us; the launch traced here: 37 us
  blocking collectives  13.1 us (35%)
  waiting for transfers between devices  10.7 us (29%)
  starting transfers between devices  7.65 us (21%)
  Pallas kernels  4.73 us (13%)
  between operations  0.69 us (2%)
    all_to_all x1, blocking collectives, swap(): boxed = lax.all_to_all(boxed, ('space', 'rep'), 0, 0, tiled=True)  13.1 us
    all_to_all x1, waiting for transfers between devices, swap(): boxed = lax.all_to_all(boxed, ('space', 'rep'), 0, 0, tiled=True)  10.7 us
    all_to_all x1, starting transfers between devices, swap(): boxed = lax.all_to_all(boxed, ('space', 'rep'), 0, 0, tiled=True)  7.33 us
    pallas_call x1, Pallas kernels, body(): pl.pallas_call(lambda *refs: route_kernel(plan, *refs), name='route', com...  2.26 us
    pallas_call x1, Pallas kernels, body(): pl.pallas_call(lambda *refs: owner_kernel(plan, *refs), name='owner', com...  1.38 us
    pallas_call x1, Pallas kernels, body(): pl.pallas_call(lambda *refs: land_kernel(plan, *refs), name='land', compi...  1.08 us
  transfers between devices with their start and end apart: 2, of which 1 were waited for; matrix products, arithmetic and copies ran while one was open for 0% of the time, Pallas kernels for 0%

profile of v5, /device:TPU:0, one launch (start us, length us, event | category | flops | bytes accessed | tf_op | source)
XLA Modules:
  0.0 37.0 jit_solution(7432658325221793654)
XLA Ops:
  0.6 0.0 copy-start
  0.6 2.3 %route.1 = (bf16[1088,128]{1,0:T(8,128)(2,1)}, s32[4,128]{1,0:T(4,128)S(1)}) custom-call(s32[1]{0:T(128)} %bitcast.refs_0_, s32[4,128]{1,0:T(4,128)} %bitcast.12, s32[4,128]{1,0:T(4,128)} %refs_2_.3, s32[4,16,128]{2,1,0:T(8,128)} %bitcast.11, s32[4,128]{1,0:T(4,128)} %refs_4_.1, s32[4,128]{1,0:T(4,128)} %refs_5_.1, bf16[4,128,128]{2,1,0:T(8,128)(2,1)} %refs_2_.5), custom_call_target="tpu_custom_call" | custom-call | tf_op jit(solution)/shard_map/route/pallas_call | solution.py:312
  2.9 7.3 %all-to-all-start = ((bf16[32,17,2,128]{3,2,1,0:T(2,128)(2,1)}), bf16[32,17,2,128]{3,2,1,0:T(2,128)(2,1)S(1)}, u32[]{:S(2)}, u32[]{:S(2)}) async-start(bf16[32,17,2,128]{3,2,1,0:T(2,128)(2,1)} %bitcast.3), calls=%async_computation | async-start | bytes 557056 | tf_op jit(solution)/shard_map/all_to_all | solution.py:301
  10.3 0.0 copy-done
  10.3 0.3 collective-permute-start
  10.6 10.7 %all-to-all-done = bf16[32,17,2,128]{3,2,1,0:T(2,128)(2,1)S(1)} async-done(((bf16[32,17,2,128]{3,2,1,0:T(2,128)(2,1)}), bf16[32,17,2,128]{3,2,1,0:T(2,128)(2,1)S(1)}, u32[]{:S(2)}, u32[]{:S(2)}) %all-to-all-start) | async-done | bytes 278560 | tf_op jit(solution)/shard_map/all_to_all | solution.py:301
  21.3 0.0 collective-permute-done.refs_3_
  21.3 1.4 %owner.1 = bf16[1088,128]{1,0:T(8,128)(2,1)S(1)} custom-call(s32[1]{0:T(128)} %bitcast.refs_0_, bf16[1088,128]{1,0:T(8,128)(2,1)S(1)} %bitcast.8, bf16[4,512,128]{2,1,0:T(8,128)(2,1)S(1)} %copy-done, bf16[4,512,128]{2,1,0:T(8,128)(2,1)S(1)} %collective-permute-done.refs_3_, bf16[8,128]{1,0:T(8,128)(2,1)S(1)} %slice_multiply_fusion.refs_4_), custom_call_target="tpu_custom_call" | custom-call | tf_op jit(solution)/shard_map/owner/pallas_call | solution.py:347
  22.7 0.0 copy-start.1
  22.7 13.1 %all_to_all.10 = bf16[32,17,2,128]{3,2,1,0:T(2,128)(2,1)S(1)} all-to-all(bf16[32,17,2,128]{3,2,1,0:T(2,128)(2,1)S(1)} %bitcast.10), channel_id=1, replica_groups=mesh['space'=16,'rep'=2] {'space','rep'}, dimensions={0} | all-to-all | bytes 557056 | tf_op jit(solution)/shard_map/all_to_all | solution.py:301
  35.9 0.0 copy-done.1
  35.9 1.1 %land.1 = (bf16[4,128,128]{2,1,0:T(8,128)(2,1)}, bf16[4,128]{1,0:T(4,128)(2,1)}) custom-call(bf16[1088,128]{1,0:T(8,128)(2,1)S(1)} %bitcast.9, s32[4,128]{1,0:T(4,128)S(1)} %get-tuple-element.5.refs_1_, bf16[4,128,128]{2,1,0:T(8,128)(2,1)S(1)} %copy-done.1), custom_call_target="tpu_custom_call" | custom-call | tf_op jit(solution)/shard_map/land/pallas_call | solution.py:356
  (1 shorter events, 0.0 us)
Async XLA Ops:
  0.6 9.6 %copy-start = (bf16[4,512,128]{2,1,0:T(8,128)(2,1)S(1)}, bf16[4,512,128]{2,1,0:T(8,128)(2,1)}, u32[]{:S(2)}) copy-start(bf16[4,512,128]{2,1,0:T(8,128)(2,1)} %refs_2_.4) | copy-start | bytes 1572868
  2.9 18.4 %all-to-all-start = ((bf16[32,17,2,128]{3,2,1,0:T(2,128)(2,1)}), bf16[32,17,2,128]{3,2,1,0:T(2,128)(2,1)S(1)}, u32[]{:S(2)}, u32[]{:S(2)}) async-start(bf16[32,17,2,128]{3,2,1,0:T(2,128)(2,1)} %bitcast.3), calls=%async_computation | async-start | bytes 557056 | tf_op jit(solution)/shard_map/all_to_all | solution.py:301
  10.3 11.1 %collective-permute-start = (bf16[4,512,128]{2,1,0:T(8,128)(2,1)S(1)}, bf16[4,512,128]{2,1,0:T(8,128)(2,1)S(1)}, u32[]{:S(2)}, u32[]{:S(2)}) collective-permute-start(bf16[4,512,128]{2,1,0:T(8,128)(2,1)S(1)} %copy-done), channel_id=1, source_target_pairs={{0,1},{1,0},{2,3},{3,2},{4,5},{5,4},{6,7},{7,6},{8,9},{9,8},{10,11... | collective-permute-start | bytes 1572872 | tf_op jit(solution)/shard_map/ppermute | solution.py:304
  22.7 13.1 %copy-start.1 = (bf16[4,128,128]{2,1,0:T(8,128)(2,1)S(1)}, bf16[4,128,128]{2,1,0:T(8,128)(2,1)}, u32[]{:S(2)}) copy-start(bf16[4,128,128]{2,1,0:T(8,128)(2,1)} %refs_2_.5) | copy-start | bytes 393220

commit v6 on v5

--- a/solution.py
+++ b/solution.py
@@ -58,24 +58,21 @@
         return (peer * self.groups + group) * size
 
 
-def route_kernel(plan, rep_ref, *refs):
-    sources, (out_ref, target_ref), held = refs[:6], refs[6:8], refs[8:14]
-    sems = refs[14]
-    copies = [pltpu.make_async_copy(x, y, sems.at[i]) for i, (x, y) in enumerate(zip(sources, held))]
-    for copy in copies:
-        copy.start()
-    owner_ref, live_ref, cand_ref, span_ref, pick_ref, rows_ref = held
+def order_kernel(plan, out_ref):
+    shape = (plan.halos, plan.halos)
+    out_ref[...] = jnp.where(iota(shape, 0) < iota(shape, 1), 1.0, 0.0).astype(jnp.bfloat16)
+
+
+def route_kernel(
+    plan, rep_ref, upper_ref, owner_ref, live_ref, cand_ref, span_ref, pick_ref, rows_ref, out_ref, target_ref
+):
     n, h, k = plan.peers, plan.halos, plan.listed
     rep = rep_ref[0]
-    upper = iota((h, h), 0) < iota((h, h), 1)
-    upper = jnp.where(upper, 1.0, 0.0).astype(jnp.bfloat16)
     peer_ids = iota((n, h), 0)
     list_ids = iota((k, h), 0)
-    for copy in copies[:-1]:
-        copy.wait()
     owners = [owner_ref[s : s + 1, :] for s in range(plan.snaps)]
     marks = jnp.concatenate([hot((n, h), 0, o) for o in owners], axis=0)
-    prefix = dot(marks, upper, 1, 0)
+    prefix = dot(marks, upper_ref[...], 1, 0)
     puts, says, spreads = [], [], []
     for s in range(plan.snaps):
         g, q = s // plan.per, s % plan.per
@@ -115,7 +112,6 @@
         return jnp.concatenate(parts[g * plan.per : (g + 1) * plan.per], axis=axis)
 
     tails = [dot(joined(says, g, 1), joined(spreads, g, 1), 1, 1) for g in range(plan.groups)]
-    copies[-1].wait()
     whole = None
     for g in range(plan.groups):
         held_rows = rows_ref[g * plan.per : (g + 1) * plan.per].reshape(plan.per * h, plan.width)
@@ -309,6 +305,14 @@
     small = pltpu.CompilerParams(vmem_limit_bytes=20 << 20)
     packed = pltpu.CompilerParams(vmem_limit_bytes=20 << 20)
     flat = (snaps, halos)
+    upper = pl.pallas_call(
+        lambda *refs: order_kernel(plan, *refs),
+        name="order",
+        compiler_params=pltpu.CompilerParams(vmem_limit_bytes=66_600_000),
+        cost_estimate=pl.CostEstimate(flops=1 << 32, bytes_accessed=0, transcendentals=0),
+        out_shape=pltpu.VMEM((halos, halos), jnp.bfloat16),
+        out_specs=vmem,
+    )()
     sent, target = pl.pallas_call(
         lambda *refs: route_kernel(plan, *refs),
         name="route",
@@ -317,30 +321,17 @@
             jax.ShapeDtypeStruct((peers * groups * plan.send, width), jnp.bfloat16),
             jax.ShapeDtypeStruct(flat, jnp.int32),
         ),
-        in_specs=[smem] + [hbm] * 6,
+        in_specs=[smem] + [vmem] * 7,
         out_specs=(vmem, vmem),
-        scratch_shapes=[
-            pltpu.VMEM(flat, jnp.int32),
-            pltpu.VMEM(flat, jnp.int32),
-            pltpu.VMEM((snaps, listed, halos), jnp.int32),
-            pltpu.VMEM(flat, jnp.int32),
-            pltpu.VMEM(flat, jnp.int32),
-            pltpu.VMEM((snaps, halos, width), jnp.bfloat16),
-            pltpu.SemaphoreType.DMA((6,)),
-        ],
     )(
         rep.reshape(1),
-        *(
-            pltpu.with_memory_space_constraint(x, pltpu.HBM)
-            for x in (
-                owner_id.reshape(flat),
-                unmatched,
-                jnp.swapaxes(cand_index, 1, 2),
-                lengths,
-                choice_index,
-                halo_rows,
-            )
-        ),
+        upper,
+        owner_id.reshape(flat),
+        unmatched,
+        jnp.swapaxes(cand_index, 1, 2),
+        lengths,
+        choice_index,
+        halo_rows,
     )
     got = swap(sent, plan.send)
     peek = got[0:SUB] * jnp.bfloat16(2)

time: 37.2 us -> 37 us (level)
  Pallas kernels: 4.73 us -> 3.69 us
  local copies, waits for them, and re-layouts: 0.01 us -> 0.84 us
    pallas_call x1, Pallas kernels: 2.26 us -> 1.22 us  [body(): pl.pallas_call(lambda *refs: route_kernel(plan, *refs), name='route', com...]
    unnamed x4 -> x14, local copies, waits for them, and re-layouts: 0.01 us -> 0.84 us
where the time goes in v6:
time: 37 us; the launch traced here: 36.8 us
  blocking collectives  13.1 us (35%)
  waiting for transfers between devices  10.7 us (29%)
  starting transfers between devices  7.64 us (21%)
  Pallas kernels  3.69 us (10%)
  local copies, waits for them, and re-layouts  0.84 us (2%)
  between operations  0.74 us (2%)
    all_to_all x1, blocking collectives, swap(): boxed = lax.all_to_all(boxed, ('space', 'rep'), 0, 0, tiled=True)  13.1 us
    all_to_all x1, waiting for transfers between devices, swap(): boxed = lax.all_to_all(boxed, ('space', 'rep'), 0, 0, tiled=True)  10.7 us
    all_to_all x1, starting transfers between devices, swap(): boxed = lax.all_to_all(boxed, ('space', 'rep'), 0, 0, tiled=True)  7.32 us
    pallas_call x1, Pallas kernels, body(): pl.pallas_call(lambda *refs: owner_kernel(plan, *refs), name='owner', com...  1.38 us
    pallas_call x1, Pallas kernels, body(): pl.pallas_call(lambda *refs: route_kernel(plan, *refs), name='route', com...  1.22 us
    pallas_call x1, Pallas kernels, body(): pl.pallas_call(lambda *refs: land_kernel(plan, *refs), name='land', compi...  1.08 us
    unnamed x14, local copies, waits for them, and re-layouts  0.84 us
  transfers between devices with their start and end apart: 2, of which 1 were waited for; matrix products, arithmetic and copies ran while one was open for 0% of the time, Pallas kernels for 0%

profile of v6, /device:TPU:0, one launch (start us, length us, event | category | flops | bytes accessed | tf_op | source)
XLA Modules:
  0.0 36.8 jit_solution(1563877325250005533)
XLA Ops:
  0.6 0.0 copy-start.1
  0.6 0.0 copy-start.2
  0.7 0.0 copy-start.3
  0.7 0.0 copy-start.4
  0.7 0.0 copy-start.5
  0.7 0.0 copy-start.6
  0.7 0.0 copy-start
  0.7 0.8 %copy-done.1 = bf16[4,128,128]{2,1,0:T(8,128)(2,1)S(1)} copy-done((bf16[4,128,128]{2,1,0:T(8,128)(2,1)S(1)}, bf16[4,128,128]{2,1,0:T(8,128)(2,1)}, u32[]{:S(2)}) %copy-start.1) | copy-done | bytes 131096
  1.5 0.0 copy-done.2
  1.5 0.0 copy-done.3
  1.5 0.0 copy-done.4
  1.5 0.0 copy-done.5
  1.6 0.0 copy-done.6
  1.6 1.2 %route.1 = (bf16[1088,128]{1,0:T(8,128)(2,1)}, s32[4,128]{1,0:T(4,128)S(1)}) custom-call(s32[1]{0:T(128)} %bitcast.refs_0_, bf16[128,128]{1,0:T(8,128)(2,1)S(1)} %order.1.refs_1_, s32[4,128]{1,0:T(4,128)S(1)} %bitcast.12, s32[4,128]{1,0:T(4,128)S(1)} %copy-done.4, s32[4,16,128]{2,1,0:T(8,128)S(1)} %bitcast.11, s32[4,128]{1,0:T(4,128)S(1)} %copy-done.5, ...), custom_call_target="tpu_custom_call" | custom-call | tf_op jit(solution)/shard_map/route/pallas_call | solution.py:316
  2.8 7.3 %all-to-all-start = ((bf16[32,17,2,128]{3,2,1,0:T(2,128)(2,1)}), bf16[32,17,2,128]{3,2,1,0:T(2,128)(2,1)S(1)}, u32[]{:S(2)}, u32[]{:S(2)}) async-start(bf16[32,17,2,128]{3,2,1,0:T(2,128)(2,1)} %bitcast.3), calls=%async_computation | async-start | bytes 557056 | tf_op jit(solution)/shard_map/all_to_all | solution.py:297
  10.1 0.0 copy-done
  10.1 0.3 collective-permute-start
  10.4 10.7 %all-to-all-done = bf16[32,17,2,128]{3,2,1,0:T(2,128)(2,1)S(1)} async-done(((bf16[32,17,2,128]{3,2,1,0:T(2,128)(2,1)}), bf16[32,17,2,128]{3,2,1,0:T(2,128)(2,1)S(1)}, u32[]{:S(2)}, u32[]{:S(2)}) %all-to-all-start) | async-done | bytes 278560 | tf_op jit(solution)/shard_map/all_to_all | solution.py:297
  21.2 0.0 collective-permute-done.refs_3_
  21.2 1.4 %owner.1 = bf16[1088,128]{1,0:T(8,128)(2,1)S(1)} custom-call(s32[1]{0:T(128)} %bitcast.refs_0_, bf16[1088,128]{1,0:T(8,128)(2,1)S(1)} %bitcast.8, bf16[4,512,128]{2,1,0:T(8,128)(2,1)S(1)} %copy-done, bf16[4,512,128]{2,1,0:T(8,128)(2,1)S(1)} %collective-permute-done.refs_3_, bf16[8,128]{1,0:T(8,128)(2,1)S(1)} %slice_multiply_fusion.refs_4_), custom_call_target="tpu_custom_call" | custom-call | tf_op jit(solution)/shard_map/owner/pallas_call | solution.py:338
  22.6 13.1 %all_to_all.10 = bf16[32,17,2,128]{3,2,1,0:T(2,128)(2,1)S(1)} all-to-all(bf16[32,17,2,128]{3,2,1,0:T(2,128)(2,1)S(1)} %bitcast.10), channel_id=1, replica_groups=mesh['space'=16,'rep'=2] {'space','rep'}, dimensions={0} | all-to-all | bytes 557056 | tf_op jit(solution)/shard_map/all_to_all | solution.py:297
  35.7 1.1 %land.1 = (bf16[4,128,128]{2,1,0:T(8,128)(2,1)}, bf16[4,128]{1,0:T(4,128)(2,1)}) custom-call(bf16[1088,128]{1,0:T(8,128)(2,1)S(1)} %bitcast.9, s32[4,128]{1,0:T(4,128)S(1)} %get-tuple-element.5.refs_1_, bf16[4,128,128]{2,1,0:T(8,128)(2,1)S(1)} %copy-done.1), custom_call_target="tpu_custom_call" | custom-call | tf_op jit(solution)/shard_map/land/pallas_call | solution.py:347
  (2 shorter events, 0.0 us)
Async XLA Ops:
  0.6 0.9 %copy-start.1 = (bf16[4,128,128]{2,1,0:T(8,128)(2,1)S(1)}, bf16[4,128,128]{2,1,0:T(8,128)(2,1)}, u32[]{:S(2)}) copy-start(bf16[4,128,128]{2,1,0:T(8,128)(2,1)} %refs_2_.3) | copy-start | bytes 393220
  0.6 0.9 %copy-start.2 = (s32[4,128,16]{1,2,0:T(8,128)S(1)}, s32[4,128,16]{1,2,0:T(8,128)}, u32[]{:S(2)}) copy-start(s32[4,128,16]{1,2,0:T(8,128)} %param.10) | copy-start | bytes 98308
  0.7 0.9 %copy-start.3 = (s32[4,128,1]{1,2,0:T(1,128)S(1)}, s32[4,128,1]{1,2,0:T(1,128)}, u32[]{:S(2)}) copy-start(s32[4,128,1]{1,2,0:T(1,128)} %param.9) | copy-start | bytes 6148
  0.7 0.9 %copy-start.4 = (s32[4,128]{1,0:T(4,128)S(1)}, s32[4,128]{1,0:T(4,128)}, u32[]{:S(2)}) copy-start(s32[4,128]{1,0:T(4,128)} %refs_3_.1) | copy-start | bytes 6148
  0.7 0.9 %copy-start.5 = (s32[4,128]{1,0:T(4,128)S(1)}, s32[4,128]{1,0:T(4,128)}, u32[]{:S(2)}) copy-start(s32[4,128]{1,0:T(4,128)} %refs_5_.1) | copy-start | bytes 6148
  0.7 0.9 %copy-start.6 = (s32[4,128]{1,0:T(4,128)S(1)}, s32[4,128]{1,0:T(4,128)}, u32[]{:S(2)}) copy-start(s32[4,128]{1,0:T(4,128)} %refs_6_.1) | copy-start | bytes 6148
  0.7 9.4 %copy-start = (bf16[4,512,128]{2,1,0:T(8,128)(2,1)S(1)}, bf16[4,512,128]{2,1,0:T(8,128)(2,1)}, u32[]{:S(2)}) copy-start(bf16[4,512,128]{2,1,0:T(8,128)(2,1)} %refs_2_.2) | copy-start | bytes 1572868
  2.8 18.4 %all-to-all-start = ((bf16[32,17,2,128]{3,2,1,0:T(2,128)(2,1)}), bf16[32,17,2,128]{3,2,1,0:T(2,128)(2,1)S(1)}, u32[]{:S(2)}, u32[]{:S(2)}) async-start(bf16[32,17,2,128]{3,2,1,0:T(2,128)(2,1)} %bitcast.3), calls=%async_computation | async-start | bytes 557056 | tf_op jit(solution)/shard_map/all_to_all | solution.py:297
  10.1 11.1 %collective-permute-start = (bf16[4,512,128]{2,1,0:T(8,128)(2,1)S(1)}, bf16[4,512,128]{2,1,0:T(8,128)(2,1)S(1)}, u32[]{:S(2)}, u32[]{:S(2)}) collective-permute-start(bf16[4,512,128]{2,1,0:T(8,128)(2,1)S(1)} %copy-done), channel_id=1, source_target_pairs={{0,1},{1,0},{2,3},{3,2},{4,5},{5,4},{6,7},{7,6},{8,9},{9,8},{10,11... | collective-permute-start | bytes 1572872 | tf_op jit(solution)/shard_map/ppermute | solution.py:300

commit v7 on v6

--- a/solution.py
+++ b/solution.py
@@ -100,7 +100,7 @@
         tells = live & (over(line, plan.codes) == rep)
         line = left(line, plan.codes)
         if plan.aligned:
-            puts.append(hot((n * plan.data, h), 0, jnp.where(live, owners[s] * plan.data + place, -1)))
+            puts.append(hot((plan.total, h), 0, jnp.where(live, owners[s] * plan.slots + rank, -1)))
             says.append(hot((n * SUB, h), 0, jnp.where(tells, owners[s] * SUB + line, -1)))
         else:
             base = plan.at(owners[s], g, plan.send)
@@ -114,16 +114,20 @@
     tails = [dot(joined(says, g, 1), joined(spreads, g, 1), 1, 1) for g in range(plan.groups)]
     whole = None
     for g in range(plan.groups):
-        held_rows = rows_ref[g * plan.per : (g + 1) * plan.per].reshape(plan.per * h, plan.width)
-        rows = dot(joined(puts, g, 1), held_rows, 1, 0)
         if plan.aligned:
-            rows, tail = rows.astype(jnp.bfloat16), tails[g].astype(jnp.bfloat16)
+            tail = tails[g].astype(jnp.bfloat16)
+            for q in range(plan.per):
+                s = g * plan.per + q
+                rows = dot(puts[s], rows_ref[s], 1, 0).astype(jnp.bfloat16)
+                for p in range(n):
+                    base = plan.at(p, g, plan.send) + q * plan.slots
+                    out_ref[base : base + plan.slots, :] = rows[p * plan.slots : (p + 1) * plan.slots]
             for p in range(n):
                 base = plan.at(p, g, plan.send)
-                out_ref[base : base + plan.data, :] = rows[p * plan.data : (p + 1) * plan.data]
                 out_ref[base + plan.data : base + plan.send, :] = tail[p * SUB : p * SUB + plan.send - plan.data]
         else:
-            both = rows + tails[g]
+            held_rows = rows_ref[g * plan.per : (g + 1) * plan.per].reshape(plan.per * h, plan.width)
+            both = dot(joined(puts, g, 1), held_rows, 1, 0) + tails[g]
             whole = both if whole is None else whole + both
     if not plan.aligned:
         out_ref[...] = whole.astype(jnp.bfloat16)
@@ -151,7 +155,7 @@
     return ref[...], (lambda p: plan.at(p, group, size) + plan.data)
 
 
-def owner_kernel(plan, rep_ref, got_ref, own_ref, other_ref, peek_ref, out_ref):
+def owner_kernel(plan, rep_ref, got_ref, own_ref, other_ref, peek_ref, out_ref, line_ref, set_ref):
     n, t, c, k = plan.peers, plan.total, plan.cands, plan.listed
     rep = rep_ref[0]
     scale = 1.0 / math.sqrt(plan.width * plan.groups)
@@ -201,16 +205,18 @@
     for q in snaps:
         index = listing[q]
         high, bit = index >> 5, jnp.left_shift(jnp.int32(1), index & (WORD - 1))
+        line_ref[q, 0], line_ref[q, 1] = high, bit
         sets = jnp.zeros((words, t), jnp.int32)
         for j in range(k):
-            sets = sets | jnp.where(high[j : j + 1, :] == word_ids, bit[j : j + 1, :], 0)
+            sets = sets | jnp.where(line_ref[q, 0, j : j + 1, :] == word_ids, line_ref[q, 1, j : j + 1, :], 0)
+        set_ref[q] = sets
         head = index[0:1, :]
         best = jnp.full((WORD, t), NEG, jnp.float32)
         picked = jnp.zeros((WORD, t), jnp.float32)
         rival = jnp.zeros((WORD, t), jnp.float32)
         for w in range(words):
             merit = merits[q][w * WORD : (w + 1) * WORD]
-            member = (sets[w : w + 1, :] & bits) != 0
+            member = (set_ref[q, w : w + 1, :] & bits) != 0
             listed = jnp.where(member, merit, NEG)
             best = jnp.maximum(best, listed)
             top = jnp.max(listed, axis=1, keepdims=True)
@@ -264,7 +270,6 @@
     h, t = plan.halos, plan.total
     target = target_ref[...]
     column = jnp.transpose(target)
-    own_row = iota((h, 1), 0) + t
     for g in range(plan.groups):
         tail, row = tail_in(plan, back_ref, g, plan.back)
         pulls = []
@@ -272,9 +277,10 @@
             s = g * plan.per + q
             spot = column[:, s : s + 1]
             owner, slot = spot >> 7, (spot & (LANES - 1)) - q * plan.slots
-            spot = jnp.where(spot >= 0, owner * plan.slots + slot, own_row)
-            rows = jnp.concatenate([rows_in(plan, back_ref, g, q, plan.back), rows_ref[s]], axis=0)
-            out_ref[s] = dot(hot((h, t + h), 1, spot), rows, 1, 0).astype(jnp.bfloat16)
+            take = hot((h, t), 1, jnp.where(spot >= 0, owner * plan.slots + slot, -1))
+            rows = dot(take, rows_in(plan, back_ref, g, q, plan.back), 1, 0)
+            rows = jnp.where(jnp.broadcast_to(spot, (h, plan.width)) >= 0, rows, rows_ref[s].astype(jnp.float32))
+            out_ref[s] = rows.astype(jnp.bfloat16)
             spot = target[s : s + 1, :]
             pulls.append(hot((tail.shape[0], h), 0, jnp.where(spot >= 0, row(spot >> 7), -1)))
         grid = dot(tail, jnp.concatenate(pulls, axis=1), 0, 0)
@@ -342,6 +348,10 @@
         out_shape=jax.ShapeDtypeStruct((peers * groups * plan.back, width), jnp.bfloat16),
         in_specs=[smem, vmem, vmem, vmem, vmem],
         out_specs=vmem,
+        scratch_shapes=[
+            pltpu.VMEM((plan.per, 2, listed, plan.total), jnp.int32),
+            pltpu.VMEM((plan.per, cands // WORD, plan.total), jnp.int32),
+        ],
     )(rep.reshape(1), got, desc_rows, other, peek)
     back = swap(reply, plan.back)
     return pl.pallas_call(

time: 37 us -> 36.9 us (level)
  no operation moved by 1% of the time
where the time goes in v7:
time: 36.9 us; the launch traced here: 36.7 us
  blocking collectives  13.1 us (36%)
  waiting for transfers between devices  10.7 us (29%)
  starting transfers between devices  7.64 us (21%)
  Pallas kernels  3.59 us (10%)
  local copies, waits for them, and re-layouts  0.84 us (2%)
  between operations  0.74 us (2%)
    all_to_all x1, blocking collectives, swap(): boxed = lax.all_to_all(boxed, ('space', 'rep'), 0, 0, tiled=True)  13.1 us
    all_to_all x1, waiting for transfers between devices, swap(): boxed = lax.all_to_all(boxed, ('space', 'rep'), 0, 0, tiled=True)  10.7 us
    all_to_all x1, starting transfers between devices, swap(): boxed = lax.all_to_all(boxed, ('space', 'rep'), 0, 0, tiled=True)  7.32 us
    pallas_call x1, Pallas kernels, body(): pl.pallas_call(lambda *refs: owner_kernel(plan, *refs), name='owner', com...  1.38 us
    pallas_call x1, Pallas kernels, body(): pl.pallas_call(lambda *refs: route_kernel(plan, *refs), name='route', com...  1.14 us
    pallas_call x1, Pallas kernels, body(): pl.pallas_call(lambda *refs: land_kernel(plan, *refs), name='land', compi...  1.06 us
    unnamed x14, local copies, waits for them, and re-layouts  0.84 us
  transfers between devices with their start and end apart: 2, of which 1 were waited for; matrix products, arithmetic and copies ran while one was open for 0% of the time, Pallas kernels for 0%

profile of v7, /device:TPU:0, one launch (start us, length us, event | category | flops | bytes accessed | tf_op | source)
XLA Modules:
  0.0 36.7 jit_solution(17021740463258210225)
XLA Ops:
  0.6 0.0 copy-start.1
  0.6 0.0 copy-start.2
  0.7 0.0 copy-start.3
  0.7 0.0 copy-start.4
  0.7 0.0 copy-start.5
  0.7 0.0 copy-start.6
  0.7 0.0 copy-start
  0.7 0.8 %copy-done.1 = bf16[4,128,128]{2,1,0:T(8,128)(2,1)S(1)} copy-done((bf16[4,128,128]{2,1,0:T(8,128)(2,1)S(1)}, bf16[4,128,128]{2,1,0:T(8,128)(2,1)}, u32[]{:S(2)}) %copy-start.1) | copy-done | bytes 131096
  1.5 0.0 copy-done.2
  1.5 0.0 copy-done.3
  1.5 0.0 copy-done.4
  1.5 0.0 copy-done.5
  1.6 0.0 copy-done.6
  1.6 1.1 %route.1 = (bf16[1088,128]{1,0:T(8,128)(2,1)}, s32[4,128]{1,0:T(4,128)S(1)}) custom-call(s32[1]{0:T(128)} %bitcast.refs_0_, bf16[128,128]{1,0:T(8,128)(2,1)S(1)} %order.1.refs_1_, s32[4,128]{1,0:T(4,128)S(1)} %bitcast.12, s32[4,128]{1,0:T(4,128)S(1)} %copy-done.4, s32[4,16,128]{2,1,0:T(8,128)S(1)} %bitcast.11, s32[4,128]{1,0:T(4,128)S(1)} %copy-done.5, ...), custom_call_target="tpu_custom_call" | custom-call | tf_op jit(solution)/shard_map/route/pallas_call | solution.py:322
  2.7 7.3 %all-to-all-start = ((bf16[32,17,2,128]{3,2,1,0:T(2,128)(2,1)}), bf16[32,17,2,128]{3,2,1,0:T(2,128)(2,1)S(1)}, u32[]{:S(2)}, u32[]{:S(2)}) async-start(bf16[32,17,2,128]{3,2,1,0:T(2,128)(2,1)} %bitcast.3), calls=%async_computation | async-start | bytes 557056 | tf_op jit(solution)/shard_map/all_to_all | solution.py:303
  10.0 0.0 copy-done
  10.0 0.3 collective-permute-start
  10.4 10.7 %all-to-all-done = bf16[32,17,2,128]{3,2,1,0:T(2,128)(2,1)S(1)} async-done(((bf16[32,17,2,128]{3,2,1,0:T(2,128)(2,1)}), bf16[32,17,2,128]{3,2,1,0:T(2,128)(2,1)S(1)}, u32[]{:S(2)}, u32[]{:S(2)}) %all-to-all-start) | async-done | bytes 278560 | tf_op jit(solution)/shard_map/all_to_all | solution.py:303
  21.1 0.0 collective-permute-done.refs_3_
  21.1 1.4 %owner.1 = bf16[1088,128]{1,0:T(8,128)(2,1)S(1)} custom-call(s32[1]{0:T(128)} %bitcast.refs_0_, bf16[1088,128]{1,0:T(8,128)(2,1)S(1)} %bitcast.8, bf16[4,512,128]{2,1,0:T(8,128)(2,1)S(1)} %copy-done, bf16[4,512,128]{2,1,0:T(8,128)(2,1)S(1)} %collective-permute-done.refs_3_, bf16[8,128]{1,0:T(8,128)(2,1)S(1)} %slice_multiply_fusion.refs_4_), custom_call_target="tpu_custom_call" | custom-call | tf_op jit(solution)/shard_map/owner/pallas_call | solution.py:344
  22.5 13.1 %all_to_all.10 = bf16[32,17,2,128]{3,2,1,0:T(2,128)(2,1)S(1)} all-to-all(bf16[32,17,2,128]{3,2,1,0:T(2,128)(2,1)S(1)} %bitcast.10), channel_id=1, replica_groups=mesh['space'=16,'rep'=2] {'space','rep'}, dimensions={0} | all-to-all | bytes 557056 | tf_op jit(solution)/shard_map/all_to_all | solution.py:303
  35.6 1.1 %land.1 = (bf16[4,128,128]{2,1,0:T(8,128)(2,1)}, bf16[4,128]{1,0:T(4,128)(2,1)}) custom-call(bf16[1088,128]{1,0:T(8,128)(2,1)S(1)} %bitcast.9, s32[4,128]{1,0:T(4,128)S(1)} %get-tuple-element.5.refs_1_, bf16[4,128,128]{2,1,0:T(8,128)(2,1)S(1)} %copy-done.1), custom_call_target="tpu_custom_call" | custom-call | tf_op jit(solution)/shard_map/land/pallas_call | solution.py:357
  (2 shorter events, 0.0 us)
Async XLA Ops:
  0.6 0.9 %copy-start.1 = (bf16[4,128,128]{2,1,0:T(8,128)(2,1)S(1)}, bf16[4,128,128]{2,1,0:T(8,128)(2,1)}, u32[]{:S(2)}) copy-start(bf16[4,128,128]{2,1,0:T(8,128)(2,1)} %refs_2_.3) | copy-start | bytes 393220
  0.6 0.9 %copy-start.2 = (s32[4,128,16]{1,2,0:T(8,128)S(1)}, s32[4,128,16]{1,2,0:T(8,128)}, u32[]{:S(2)}) copy-start(s32[4,128,16]{1,2,0:T(8,128)} %param.10) | copy-start | bytes 98308
  0.7 0.9 %copy-start.3 = (s32[4,128,1]{1,2,0:T(1,128)S(1)}, s32[4,128,1]{1,2,0:T(1,128)}, u32[]{:S(2)}) copy-start(s32[4,128,1]{1,2,0:T(1,128)} %param.9) | copy-start | bytes 6148
  0.7 0.9 %copy-start.4 = (s32[4,128]{1,0:T(4,128)S(1)}, s32[4,128]{1,0:T(4,128)}, u32[]{:S(2)}) copy-start(s32[4,128]{1,0:T(4,128)} %refs_3_.1) | copy-start | bytes 6148
  0.7 0.9 %copy-start.5 = (s32[4,128]{1,0:T(4,128)S(1)}, s32[4,128]{1,0:T(4,128)}, u32[]{:S(2)}) copy-start(s32[4,128]{1,0:T(4,128)} %refs_5_.1) | copy-start | bytes 6148
  0.7 0.9 %copy-start.6 = (s32[4,128]{1,0:T(4,128)S(1)}, s32[4,128]{1,0:T(4,128)}, u32[]{:S(2)}) copy-start(s32[4,128]{1,0:T(4,128)} %refs_6_.1) | copy-start | bytes 6148
  0.7 9.3 %copy-start = (bf16[4,512,128]{2,1,0:T(8,128)(2,1)S(1)}, bf16[4,512,128]{2,1,0:T(8,128)(2,1)}, u32[]{:S(2)}) copy-start(bf16[4,512,128]{2,1,0:T(8,128)(2,1)} %refs_2_.2) | copy-start | bytes 1572868
  2.7 18.4 %all-to-all-start = ((bf16[32,17,2,128]{3,2,1,0:T(2,128)(2,1)}), bf16[32,17,2,128]{3,2,1,0:T(2,128)(2,1)S(1)}, u32[]{:S(2)}, u32[]{:S(2)}) async-start(bf16[32,17,2,128]{3,2,1,0:T(2,128)(2,1)} %bitcast.3), calls=%async_computation | async-start | bytes 557056 | tf_op jit(solution)/shard_map/all_to_all | solution.py:303
  10.0 11.1 %collective-permute-start = (bf16[4,512,128]{2,1,0:T(8,128)(2,1)S(1)}, bf16[4,512,128]{2,1,0:T(8,128)(2,1)S(1)}, u32[]{:S(2)}, u32[]{:S(2)}) collective-permute-start(bf16[4,512,128]{2,1,0:T(8,128)(2,1)S(1)} %copy-done), channel_id=1, source_target_pairs={{0,1},{1,0},{2,3},{3,2},{4,5},{5,4},{6,7},{7,6},{8,9},{9,8},{10,11... | collective-permute-start | bytes 1572872 | tf_op jit(solution)/shard_map/ppermute | solution.py:306
